TPU v7x, 32 devices: a whole 2x2x4 slice. The times are simulated.
32 devices in a mesh: grp: 2 (over x), space: 16 (over z, y, core).
Axes of the slice: x: 2, y: 2, z: 4, core: 2. Of those that a mesh axis runs over, the one named last changes fastest.
Arguments:
- propagator: bfloat16 [4, 3, 4, 12, 32768], P('grp', None, None, None, 'space'), parts along dimension 0, may hold values from -6 to 6
- eigvecs: bfloat16 [4, 3, 256, 32768], P('grp', None, None, 'space'), parts along dimension 0, may hold values from -6 to 6
- operator_weights: float32 [256, 2, 256], P('grp'), parts along dimension 0, may hold values from -0.375 to 0.375
- sink_time: int32 [2], P('grp'), parts along dimension 0, may hold values from 0 to 127
- term_index: int32 [48, 3], replicated, may hold values from 0 to 11
- term_sign: int32 [48], replicated, may hold values from 0 to 1
- solver_order: int32 [32768], P('space'), may hold values from 0 to 32767, as said below
Outputs:
- solver_source: bfloat16 [4, 3, 4, 12, 32768], P('grp', None, None, None, 'space'), parts along dimension 0
There are 2 independent parts, one for each index of `grp`. A program takes and returns all parts, laid end to end along the dimension named above; an argument that names none is the same for every part. Nothing has to cross between parts.
Inputs may be any that keep to these rules, and one draw needn't show every extreme that they name: solver_order is a permutation of the sites; split into blocks of 2048 positions and each block into pieces of 128, piece d of block e holds only sites d * 2048 to (d + 1) * 2048 - 1.
All inputs are finite; a program needn't handle non-finite values.
Results may differ from a plain program's by a relative error of at most 0.006.
Values may be sent and summed in bfloat16 or wider, within the bound.
A program may use at most 64 MiB of HBM per device.

v0:
```python
import functools
import math

import jax
import jax.numpy as jnp
from jax import lax
from jax.experimental import pallas as pl
from jax.experimental.pallas import tpu as pltpu
from jax.sharding import PartitionSpec as P

NMOM = 4
EXTENT = 64
MOMENTA = ((0, 0, 0), (1, 0, 0), (0, 1, 0), (0, 0, 1))
HIGH = lax.Precision.HIGHEST
F32 = jnp.float32
BF16 = jnp.bfloat16
MESH = pl.DeviceIdType.MESH


def swap_halves(x):
    top, bottom = x[..., :4, :], x[..., 4:, :]
    return jnp.concatenate([-bottom, top], axis=-2)


def dot32(a, b):
    return jnp.dot(a, b, precision=HIGH, preferred_element_type=F32)


def kernel(
    n, units, columns, scale_in, scale_out, chunk,
    prop, eig_hbm, sink, table_weights, term_rows, term_sign, order, out,
    eig, trig, acc, blocks, from_core, summed, from_chips, coeffs, lhs, source, wanted, onehot,
    staged, eig_sem, core_send, core_recv, chip_send, chip_recv, all_send, all_recv,
    fwd_send, fwd_recv, index_send, index_recv, out_send, out_recv, own_sem,
):
    me = lax.axis_index("space")
    chips = n // 2
    core = lax.rem(me, 2)
    chip = me // 2
    partner = me + 1 - 2 * core
    length = eig.shape[-1]
    nvec = eig.shape[2]
    piece = order.shape[-1]
    filled = NMOM * columns // (2 * units)
    steps = length // chunk
    rows = NMOM * columns * 8

    def each(lower, upper, body):
        def step(i, carry):
            body(i)
            return carry

        lax.fori_loop(lower, upper, step, 0)

    def remote(src, dst, send_sem, recv_sem, device):
        return pltpu.make_async_remote_copy(
            src_ref=src, dst_ref=dst, send_sem=send_sem, recv_sem=recv_sem,
            device_id={"space": device}, device_id_type=MESH,
        )

    loads = []
    for colour in range(3):
        load = pltpu.make_async_copy(eig_hbm.at[:, colour], eig.at[:, colour], eig_sem.at[colour])
        load.start()
        loads.append(load)

    barrier = pltpu.get_barrier_semaphore()
    each(1, n, lambda t: pl.semaphore_signal(
        barrier, inc=1, device_id={"space": lax.rem(me + t, n)}, device_id_type=MESH
    ))

    site = me * length + lax.broadcasted_iota(jnp.int32, (1, length), 1)
    bits = EXTENT.bit_length() - 1
    low = EXTENT - 1
    coords = (site & low, (site >> bits) & low, site >> (2 * bits))
    for p in range(1, NMOM):
        winding = sum(step * coord for step, coord in zip(MOMENTA[p], coords) if step) & low
        angle = winding.astype(F32) * (2.0 * math.pi / EXTENT)
        trig[p : p + 1, :] = jnp.cos(angle)
        trig[NMOM + p : NMOM + p + 1, :] = jnp.sin(angle)
    terms = term_rows.shape[1]
    eye = lax.broadcasted_iota(jnp.int32, (terms, terms), 0) == lax.broadcasted_iota(
        jnp.int32, (terms, terms), 1
    )
    lane = lax.broadcasted_iota(jnp.int32, (terms, 24), 1)
    lane_channel = (4 * (lane >> 3) + (lane & 3)).astype(F32)
    lane_imag = (lane >> 2) & 1
    picks = []
    for which in range(2):
        row = term_rows[which : which + 1, :].astype(F32)
        column = jnp.sum(jnp.where(eye, row, 0.0), axis=1, keepdims=True)
        for part in range(2):
            hit = (lane_channel == column) & (lane_imag == part)
            picks.append(jnp.where(hit, 1.0, 0.0))
    picks = jnp.concatenate(picks)
    sub = lax.broadcasted_iota(jnp.int32, (24, terms), 0)
    target = 4 * (sub >> 3) + (sub & 3) == term_rows[2:3, :]
    signs = (2 * term_sign[...] - 1).astype(F32)
    place_real = jnp.where(target & (((sub >> 2) & 1) == 0), signs, 0.0)
    place_imag = jnp.where(target & (((sub >> 2) & 1) == 1), signs, 0.0)
    time_index = lax.broadcasted_iota(jnp.int32, table_weights.shape, 0)
    weights = jnp.sum(jnp.where(time_index == sink[0], table_weights[...], 0.0), axis=0)
    weight_real, weight_imag = weights[0:1, :], weights[1:2, :]

    if filled < chips:
        blocks[:, filled:] = jnp.zeros((3, chips - filled) + blocks.shape[2:], F32)

    def index_copy(peer, dst, sem_slot):
        return remote(
            order.at[peer], wanted.at[dst], index_send.at[peer], index_recv.at[sem_slot], peer
        )

    def core_copy(colour):
        return remote(
            blocks.at[colour, :, 1 - core], from_core.at[colour],
            core_send.at[colour], core_recv.at[colour], partner,
        )

    def chip_copy(colour, other, dst):
        return remote(
            summed.at[colour, other], from_chips.at[colour, dst],
            chip_send.at[colour, other], chip_recv.at[colour, dst], other * 2 + core,
        )

    def send_sums(colour):
        core_copy(colour).wait()

        def send(t):
            other = lax.rem(chip + t, chips)
            summed[colour, pl.ds(other, 1)] = (
                blocks[colour, pl.ds(other, 1), pl.ds(core, 1)][:, 0]
                + from_core[colour, pl.ds(other, 1)]
            ).astype(BF16)
            chip_copy(colour, other, chip).start()

        each(1, chips, send)

    for colour in range(3):
        loads[colour].wait()
        acc[...] = jnp.zeros_like(acc)

        def project(step, colour=colour):
            sites = pl.ds(pl.multiple_of(step * chunk, chunk), chunk)
            real = prop[0, colour, :, :, sites].astype(F32)
            imag = prop[1, colour, :, :, sites].astype(F32)
            straight = jnp.concatenate([real, imag], axis=1)
            crossed = jnp.concatenate([imag, -real], axis=1)
            first, second = [straight], [crossed]
            for p in range(1, NMOM):
                cosine = trig[p : p + 1, sites][None]
                sine = trig[NMOM + p : NMOM + p + 1, sites][None]
                first.append(cosine * straight + sine * crossed)
                second.append(cosine * crossed - sine * straight)
            first = jnp.concatenate(first).reshape(rows, chunk).astype(BF16)
            second = jnp.concatenate(second).reshape(rows, chunk).astype(BF16)
            dims = (((1,), (1,)), ((), ()))
            acc[...] += lax.dot_general(
                first, eig[0, colour, :, sites], dims, preferred_element_type=F32
            ) + lax.dot_general(
                second, eig[1, colour, :, sites], dims, preferred_element_type=F32
            )

        each(0, steps, project)
        blocks[colour, :filled] = (acc[...] * scale_in).reshape(filled, 2, units, 8, nvec)
        if colour == 0:
            pl.semaphore_wait(barrier, n - 1)
            core_copy(0).start()

            def send_index(t):
                peer = lax.rem(me + t, n)
                index_copy(peer, me, me).start()

            each(1, n, send_index)
            wanted[pl.ds(me, 1)] = order[pl.ds(me, 1)]
        else:
            core_copy(colour).start()
            send_sums(colour - 1)
    send_sums(2)

    def index_in(t):
        other = lax.rem(me + t, n)
        index_copy(other, other, other).wait_recv()

    each(1, n, index_in)

    def build(peer_chip):
        position = lax.broadcasted_iota(jnp.int32, (length, piece), 0)
        for half in range(2):
            local = wanted[pl.ds(peer_chip * 2 + half, 1)][0] - me * length
            onehot[pl.ds(peer_chip, 1), :, half * piece : (half + 1) * piece] = jnp.where(
                position == local, 1.0, 0.0
            ).astype(BF16)[None]

    each(0, chips, build)

    totals = []
    for colour in range(3):
        own = blocks[colour, pl.ds(chip, 1), pl.ds(core, 1)][:, 0]
        own = (own + from_core[colour, pl.ds(chip, 1)]).reshape(units * 8, nvec)

        def add_sum(t, total, colour=colour):
            other = lax.rem(chip + chips - t, chips)
            chip_copy(colour, other, other).wait_recv()
            part = from_chips[colour, pl.ds(other, 1)].astype(F32)
            return total + part.reshape(units * 8, nvec)

        totals.append(lax.fori_loop(1, chips, add_sum, own))

    for unit in range(units):
        block = jnp.concatenate([total[unit * 8 : (unit + 1) * 8] for total in totals])
        picked = dot32(picks, block)
        first_real, first_imag = picked[:terms], picked[terms : 2 * terms]
        other_real, other_imag = picked[2 * terms : 3 * terms], picked[3 * terms :]
        second_real = jnp.sum(
            weight_real * other_real - weight_imag * other_imag, axis=1, keepdims=True
        )
        second_imag = jnp.sum(
            weight_real * other_imag + weight_imag * other_real, axis=1, keepdims=True
        )
        made = dot32(place_real, first_real * second_real - first_imag * second_imag) + dot32(
            place_imag, first_real * second_imag + first_imag * second_real
        )
        made = made.reshape(3, 8, nvec).astype(BF16)
        for colour in range(3):
            coeffs[colour, pl.ds(me, 1), unit] = made[colour : colour + 1]

    def gather_copy(colour, slot, other, device):
        return remote(
            coeffs.at[colour, slot], coeffs.at[colour, slot],
            all_send.at[colour, other], all_recv.at[colour, slot // 2], device,
        )

    def forward_copy(colour, slot):
        return remote(
            coeffs.at[colour, slot], coeffs.at[colour, slot],
            fwd_send.at[colour, slot // 2], fwd_recv.at[colour, slot // 2], partner,
        )

    for colour in range(3):
        def send_coeffs(t, colour=colour):
            other = lax.rem(chip + t, chips)
            gather_copy(colour, me, other, other * 2 + core).start()

        each(1, chips, send_coeffs)
        forward_copy(colour, me).start()

    def relay(colour):
        def pass_on(t):
            other = lax.rem(chip + chips - t, chips)
            slot = other * 2 + core
            gather_copy(colour, slot, other, slot).wait_recv()
            forward_copy(colour, slot).start()

        each(1, chips, pass_on)

    def out_copy(colour, slot, device, dst, sem_slot):
        return remote(
            staged.at[slot, colour], out.at[dst, colour],
            out_send.at[colour, slot], out_recv.at[colour, sem_slot], device,
        )

    def keep(colour):
        return pltpu.make_async_copy(
            staged.at[me, colour], out.at[me, colour], own_sem.at[colour]
        )

    relay(0)
    for colour in range(3):
        each(0, chips, lambda c, colour=colour: forward_copy(colour, c * 2 + 1 - core).wait_recv())
        table = coeffs[colour].astype(F32).reshape(n * units, 8, nvec)[: NMOM * columns]
        lhs[0] = table.reshape(rows, nvec).astype(BF16)
        lhs[1] = swap_halves(table).reshape(rows, nvec).astype(BF16)

        def rebuild(step, colour=colour):
            sites = pl.ds(pl.multiple_of(step * chunk, chunk), chunk)
            grid = jnp.dot(
                lhs[0], eig[0, colour, :, sites], preferred_element_type=F32
            ) + jnp.dot(lhs[1], eig[1, colour, :, sites], preferred_element_type=F32)
            grid = grid.reshape(NMOM, columns, 8, chunk)
            straight, crossed = grid[0], None
            for p in range(1, NMOM):
                straight = straight + trig[p : p + 1, sites][None] * grid[p]
                turned = trig[NMOM + p : NMOM + p + 1, sites][None] * grid[p]
                crossed = turned if crossed is None else crossed + turned
            made = (straight + swap_halves(crossed)) * scale_out
            source[:, sites] = made.reshape(columns * 8, chunk).astype(BF16)

        each(0, steps, rebuild)
        if colour < 2:
            relay(colour + 1)

        def choose(peer_chip, colour=colour):
            chosen = jnp.dot(
                source[...], onehot[pl.ds(peer_chip, 1)][0], preferred_element_type=F32
            ).astype(BF16)
            for half in range(2):
                staged[pl.ds(peer_chip * 2 + half, 1), colour] = chosen[
                    :, half * piece : (half + 1) * piece
                ][None]

        def send_pieces(t, colour=colour):
            other = lax.rem(chip + t, chips)
            choose(other)
            for half in range(2):
                peer = other * 2 + half
                out_copy(colour, peer, peer, me, me).start()

        each(1, chips, send_pieces)
        choose(chip)
        out_copy(colour, partner, partner, me, me).start()
        keep(colour).start()

    def close_index(t):
        peer = lax.rem(me + t, n)
        index_copy(peer, me, me).wait_send()

    each(1, n, close_index)
    for colour in range(3):
        def close(t, colour=colour):
            peer = lax.rem(me + t, n)
            out_copy(colour, peer, peer, me, me).wait_send()

        def close_chips(t, colour=colour):
            other = lax.rem(chip + t, chips)
            chip_copy(colour, other, chip).wait_send()
            gather_copy(colour, me, other, other * 2 + core).wait_send()

        def take_piece(t, colour=colour):
            peer = lax.rem(me + n - t, n)
            out_copy(colour, peer, peer, peer, peer).wait_recv()

        each(1, chips, close_chips)
        each(0, chips, lambda c, colour=colour: forward_copy(colour, c * 2 + core).wait_send())
        each(1, n, close)
        each(1, n, take_piece)
        keep(colour).wait()


def on_device(
    propagator, eigvecs, operator_weights, sink_time, term_index, term_sign, solver_order
):
    columns, length = propagator.shape[3:]
    nvec = eigvecs.shape[2]
    n = lax.axis_size("space")
    chips = n // 2
    piece = length // n
    units = -(-NMOM * columns // n)
    rows = NMOM * columns * 8
    site_rows = columns * 8
    unit = (units, 8, nvec)
    vmem = pl.BlockSpec(memory_space=pltpu.VMEM)
    smem = pl.BlockSpec(memory_space=pltpu.SMEM)
    hbm = pl.BlockSpec(memory_space=pl.ANY)
    dma = pltpu.SemaphoreType.DMA
    gathered = pl.pallas_call(
        functools.partial(
            kernel, n, units, columns, 1.0 / math.sqrt(3.0 * length * n),
            1.0 / math.sqrt(NMOM * nvec), 512,
        ),
        out_shape=jax.ShapeDtypeStruct((n, 3, site_rows, piece), BF16),
        in_specs=[vmem, hbm, smem, vmem, vmem, vmem, vmem],
        out_specs=hbm,
        scratch_shapes=[
            pltpu.VMEM(eigvecs.shape, BF16),
            pltpu.VMEM((2 * NMOM, length), F32),
            pltpu.VMEM((rows, nvec), F32),
            pltpu.VMEM((3, chips, 2) + unit, F32),
            pltpu.VMEM((3, chips) + unit, F32),
            pltpu.VMEM((3, chips) + unit, BF16),
            pltpu.VMEM((3, chips) + unit, BF16),
            pltpu.VMEM((3, n) + unit, BF16),
            pltpu.VMEM((2, rows, nvec), BF16),
            pltpu.VMEM((site_rows, length), BF16),
            pltpu.VMEM((n, 1, piece), jnp.int32),
            pltpu.VMEM((chips, length, 2 * piece), BF16),
            pltpu.VMEM((n, 3, site_rows, piece), BF16),
            dma((3,)), dma((3,)), dma((3,)), dma((3, chips)), dma((3, chips)), dma((3, chips)),
            dma((3, chips)), dma((3, chips)), dma((3, chips)), dma((n,)), dma((n,)),
            dma((3, n)), dma((3, n)), dma((3,)),
        ],
        compiler_params=pltpu.CompilerParams(
            collective_id=0, has_side_effects=True, vmem_limit_bytes=60 * 2**20
        ),
    )(
        propagator.transpose(0, 1, 3, 2, 4), eigvecs, sink_time, operator_weights,
        term_index.T, term_sign.reshape(1, -1), solver_order.reshape(n, 1, piece),
    )
    placed = gathered.reshape(n, 3, columns, 2, 4, piece).transpose(3, 1, 4, 2, 0, 5)
    return placed.reshape(2, 3, 4, columns, length)


def solution(mesh):
    return jax.shard_map(
        on_device,
        mesh=mesh,
        in_specs=(
            P("grp", None, None, None, "space"),
            P("grp", None, None, "space"),
            P("grp", None, None),
            P("grp"),
            P(),
            P(),
            P("space"),
        ),
        out_specs=P("grp", None, None, None, "space"),
        check_vma=False,
    )
```

profile of v0, /device:TPU:0, one launch (start us, length us, event | category | flops | bytes accessed | tf_op | source)
XLA Modules:
  0.0 60.1 jit_solution(12444569567358190668)
XLA Ops:
  0.7 56.2 %shard_map.73 = bf16[16,3,96,128]{3,2,1,0:T(8,128)(2,1)} custom-call(bf16[2,3,12,4,2048]{4,3,2,1,0:T(4,128)(2,1)} %bitcast.12, bf16[2,3,256,2048]{3,2,1,0:T(8,128)(2,1)} %eig_hbm.1, s32[1]{0:T(128)S(6)} %copy.9.sink, f32[128,2,256]{2,1,0:T(2,128)} %table_weights.1, s32[3,48]{1,0:T(4,128)} %bitcast.14, s32[1,48]{1,0:T(1,128)} %bitcast.15, s32[16,1,128]{2,1,0:T(1,128)} %bitcast.13), custom_call_target="tpu_custom_call" | custom-call | tf_op jit(solution)/shard_map/pallas_call | solution.py:355
  56.9 2.0 %copy.8 = bf16[2,3,4,12,16,128]{5,4,2,3,1,0:T(8,128)(2,1)S(1)} copy(bf16[2,3,4,12,16,128]{5,2,0,3,1,4:T(4,128)(2,1)} %bitcast.11) | data formatting | bytes 2359296 | tf_op jit(solution)/shard_map/transpose | solution.py:388
  58.9 1.2 %reshape.15 = bf16[2,3,4,12,2048]{4,2,3,1,0:T(4,128)(2,1)} reshape(bf16[2,3,4,12,16,128]{5,4,2,3,1,0:T(8,128)(2,1)S(1)} %copy.8) | data formatting | bytes 2359296 | tf_op jit(solution)/shard_map/reshape | solution.py:389
where the time goes:
time: 60.6 us; the launch traced here: 60.1 us
  Pallas kernels  56.2 us (93%)
  local copies, waits for them, and re-layouts  3.2 us (5%)
  between operations  0.66 us (1%)
    pallas_call x1, Pallas kernels, on_device(): pl.pallas_call(functools.partial(kernel, n, units, columns, 1.0 / math.sq...  56.2 us
    transpose x1, local copies, waits for them, and re-layouts, on_device(): gathered.reshape(n, 3, columns, 2, 4, piece).transpose(3, 1, 4, 2, 0, 5)  2.03 us

commit v1 on v0

v1 whole, which is shorter than its diff:
```python
import functools
import math

import jax
import jax.numpy as jnp
from jax import lax
from jax.experimental import pallas as pl
from jax.experimental.pallas import tpu as pltpu
from jax.sharding import PartitionSpec as P

NMOM = 4
EXTENT = 64
MOMENTA = ((0, 0, 0), (1, 0, 0), (0, 1, 0), (0, 0, 1))
F32 = jnp.float32
BF16 = jnp.bfloat16
MESH = pl.DeviceIdType.MESH


def swap_halves(x):
    top, bottom = x[..., :4, :], x[..., 4:, :]
    return jnp.concatenate([-bottom, top], axis=-2)


def dot_exact(a, b):
    high = b.astype(BF16)
    low = (b - high.astype(F32)).astype(BF16)
    return jnp.dot(a, high, preferred_element_type=F32) + jnp.dot(a, low, preferred_element_type=F32)


def kernel(
    n, units, columns, scale_in, scale_out, chunk, moving, fixed, direct,
    prop_hbm, eig_hbm, sink, table_hbm, term_rows, term_sign, order, out,
    prop, eig, table_weights, trig, acc, blocks, from_core, summed, from_chips, coeffs, lhs,
    source, wanted, onehot, staged,
    load_sem, core_recv, chip_recv, all_recv, fwd_recv, sems,
):
    me = lax.axis_index("space")
    chips = n // 2
    half = chips // 2
    core = lax.rem(me, 2)
    chip = me // 2
    side = chip // half
    partner = me + 1 - 2 * core
    length = eig.shape[-1]
    nvec = eig.shape[2]
    piece = order.shape[-1]
    filled = NMOM * columns // (2 * units)
    steps = length // chunk
    plan = (0,) + moving
    base_rows = columns * 8
    rows = len(plan) * base_rows
    core_send, chip_send, all_send, fwd_send, index_send, index_recv, out_send, out_recv, own_sem = (
        sems.at[i] for i in range(9)
    )

    def each(lower, upper, body):
        def step(i, carry):
            body(i)
            return carry

        lax.fori_loop(lower, upper, step, 0)

    def far_chips(body):
        each(0, half, lambda t: body((1 - side) * half + lax.rem(chip + t, half)))

    def near_chips(body):
        each(1, half, lambda t: body(side * half + lax.rem(chip + t, half)))

    def remote(src, dst, send_sem, recv_sem, device):
        return pltpu.make_async_remote_copy(
            src_ref=src, dst_ref=dst, send_sem=send_sem, recv_sem=recv_sem,
            device_id={"space": device}, device_id_type=MESH,
        )

    def sent(ref, sem):
        remote(ref, ref, sem, sem, partner).wait_send()

    def landed(ref, sem):
        remote(ref, ref, sem, sem, partner).wait_recv()

    loads = []
    for colour in range(3):
        pair = (
            pltpu.make_async_copy(prop_hbm.at[:, colour], prop.at[:, colour], load_sem.at[colour]),
            pltpu.make_async_copy(eig_hbm.at[:, colour], eig.at[:, colour], load_sem.at[3 + colour]),
        )
        for load in pair:
            load.start()
        loads.append(pair)
    table_load = pltpu.make_async_copy(table_hbm, table_weights, load_sem.at[6])
    table_load.start()

    barrier = pltpu.get_barrier_semaphore()
    each(1, n, lambda t: pl.semaphore_signal(
        barrier, inc=1, device_id={"space": lax.rem(me + t, n)}, device_id_type=MESH
    ))

    bits = EXTENT.bit_length() - 1
    low = EXTENT - 1

    def angles(p, site):
        coords = (site & low, (site >> bits) & low, site >> (2 * bits))
        winding = sum(step * coord for step, coord in zip(MOMENTA[p], coords) if step) & low
        return winding.astype(F32) * (2.0 * math.pi / EXTENT)

    tiles = length // 128
    compact = me * length + 128 * lax.broadcasted_iota(
        jnp.int32, (tiles, 128), 0
    ) + lax.broadcasted_iota(jnp.int32, (tiles, 128), 1)
    for slot, p in enumerate(moving):
        angle = angles(p, compact)
        for part, values in enumerate((jnp.cos(angle), jnp.sin(angle))):
            trig[2 * slot + part : 2 * slot + part + 1, :] = jnp.concatenate(
                [values[tile : tile + 1] for tile in range(tiles)], axis=1
            )
    turns = []
    for p in fixed:
        angle = angles(p, me * length + jnp.zeros((1, nvec), jnp.int32))
        turns.append((jnp.cos(angle)[None], jnp.sin(angle)[None]))

    if filled < chips:
        blocks[:, filled:] = jnp.zeros((3, chips - filled) + blocks.shape[2:], F32)

    def core_copy(colour):
        return remote(
            blocks.at[colour, :, 1 - core], from_core.at[colour], core_send,
            core_recv.at[colour], partner,
        )

    def send_sums(colour):
        core_copy(colour).wait_recv()

        def send(other):
            summed[colour, pl.ds(other, 1)] = (
                blocks[colour, pl.ds(other, 1), pl.ds(core, 1)][:, 0]
                + from_core[colour, pl.ds(other, 1)]
            ).astype(BF16)
            remote(
                summed.at[colour, other], from_chips.at[colour, chip], chip_send,
                chip_recv.at[colour], other * 2 + core,
            ).start()

        far_chips(send)
        near_chips(send)

    for colour in range(3):
        for load in loads[colour]:
            load.wait()
        acc[...] = jnp.zeros_like(acc)

        def project(step, colour=colour):
            sites = pl.ds(pl.multiple_of(step * chunk, chunk), chunk)
            real = prop[0, colour, :, :, sites].astype(F32)
            imag = prop[1, colour, :, :, sites].astype(F32)
            straight = jnp.concatenate([real, imag], axis=1)
            crossed = jnp.concatenate([imag, -real], axis=1)
            first, second = [straight], [crossed]
            for slot in range(len(moving)):
                cosine = trig[2 * slot : 2 * slot + 1, sites][None]
                sine = trig[2 * slot + 1 : 2 * slot + 2, sites][None]
                first.append(cosine * straight + sine * crossed)
                second.append(cosine * crossed - sine * straight)
            first = jnp.concatenate(first).reshape(rows, chunk).astype(BF16)
            second = jnp.concatenate(second).reshape(rows, chunk).astype(BF16)
            dims = (((1,), (1,)), ((), ()))
            acc[...] += lax.dot_general(
                first, eig[0, colour, :, sites], dims, preferred_element_type=F32
            ) + lax.dot_general(
                second, eig[1, colour, :, sites], dims, preferred_element_type=F32
            )

        each(0, steps, project)
        made = (acc[...] * scale_in).reshape(len(plan) * columns, 8, nvec)
        still = made[:columns]
        crossed = swap_halves(still)
        made = jnp.concatenate(
            [made] + [cosine * still - sine * crossed for cosine, sine in turns]
        )
        blocks[colour, :filled] = made.reshape(filled, 2, units, 8, nvec)
        if colour == 0:
            pl.semaphore_wait(barrier, n - 1)
            core_copy(0).start()

            def send_index(t):
                peer = lax.rem(me + t, n)
                remote(order.at[peer], wanted.at[me], index_send, index_recv, peer).start()

            each(1, n, send_index)
            wanted[pl.ds(me, 1)] = order[pl.ds(me, 1)]
        else:
            core_copy(colour).start()
            send_sums(colour - 1)
    send_sums(2)

    landed(wanted.at[pl.ds(0, n - 1)], index_recv)

    def build(peer_chip):
        position = lax.broadcasted_iota(jnp.int32, (length, piece), 0)
        for which in range(2):
            local = wanted[pl.ds(peer_chip * 2 + which, 1)][0] - me * length
            onehot[pl.ds(peer_chip, 1), :, which * piece : (which + 1) * piece] = jnp.where(
                position == local, 1.0, 0.0
            ).astype(BF16)[None]

    each(0, chips, build)

    terms = term_rows.shape[1]
    eye = lax.broadcasted_iota(jnp.int32, (terms, terms), 0) == lax.broadcasted_iota(
        jnp.int32, (terms, terms), 1
    )
    lane = lax.broadcasted_iota(jnp.int32, (terms, 24), 1)
    lane_channel = (4 * (lane >> 3) + (lane & 3)).astype(F32)
    lane_imag = (lane >> 2) & 1
    picks = []
    for which in range(2):
        row = term_rows[which : which + 1, :].astype(F32)
        column = jnp.sum(jnp.where(eye, row, 0.0), axis=1, keepdims=True)
        for part in range(2):
            hit = (lane_channel == column) & (lane_imag == part)
            picks.append(jnp.where(hit, 1.0, 0.0))
    picks = jnp.concatenate(picks).astype(BF16)
    sub = lax.broadcasted_iota(jnp.int32, (24, terms), 0)
    target = 4 * (sub >> 3) + (sub & 3) == term_rows[2:3, :]
    signs = (2 * term_sign[...] - 1).astype(F32)
    place_real = jnp.where(target & (((sub >> 2) & 1) == 0), signs, 0.0).astype(BF16)
    place_imag = jnp.where(target & (((sub >> 2) & 1) == 1), signs, 0.0).astype(BF16)
    table_load.wait()
    weights = table_weights[sink[0]]
    weight_real, weight_imag = weights[0:1, :], weights[1:2, :]

    totals = []
    for colour in range(3):
        own = blocks[colour, pl.ds(chip, 1), pl.ds(core, 1)][:, 0]
        own = (own + from_core[colour, pl.ds(chip, 1)]).reshape(units * 8, nvec)
        landed(from_chips.at[colour, pl.ds(0, chips - 1)], chip_recv.at[colour])

        def add_sum(t, total, colour=colour):
            other = lax.rem(chip + chips - t, chips)
            part = from_chips[colour, pl.ds(other, 1)].astype(F32)
            return total + part.reshape(units * 8, nvec)

        totals.append(lax.fori_loop(1, chips, add_sum, own))

    block = jnp.concatenate([
        jnp.concatenate([total[unit * 8 : (unit + 1) * 8] for total in totals])
        for unit in range(units)
    ], axis=1)
    picked = dot_exact(picks, block)
    first_real, first_imag = picked[:terms], picked[terms : 2 * terms]
    other_real, other_imag = picked[2 * terms : 3 * terms], picked[3 * terms :]
    real_products, imag_products = [], []
    for unit in range(units):
        lanes = slice(unit * nvec, (unit + 1) * nvec)
        o_real, o_imag = other_real[:, lanes], other_imag[:, lanes]
        f_real, f_imag = first_real[:, lanes], first_imag[:, lanes]
        second_real = jnp.sum(weight_real * o_real - weight_imag * o_imag, axis=1, keepdims=True)
        second_imag = jnp.sum(weight_real * o_imag + weight_imag * o_real, axis=1, keepdims=True)
        real_products.append(f_real * second_real - f_imag * second_imag)
        imag_products.append(f_real * second_imag + f_imag * second_real)
    made = dot_exact(place_real, jnp.concatenate(real_products, axis=1)) + dot_exact(
        place_imag, jnp.concatenate(imag_products, axis=1)
    )
    for unit in range(units):
        part = made[:, unit * nvec : (unit + 1) * nvec].reshape(3, 8, nvec).astype(BF16)
        for colour in range(3):
            coeffs[colour, pl.ds(core, 1), pl.ds(chip, 1), unit] = part[colour : colour + 1][None]

    for colour in range(3):
        def send_coeffs(other, colour=colour):
            remote(
                coeffs.at[colour, core, chip], coeffs.at[colour, core, chip], all_send,
                all_recv.at[colour], other * 2 + core,
            ).start()

        far_chips(send_coeffs)
        near_chips(send_coeffs)

    def relay(colour):
        landed(coeffs.at[colour, core, pl.ds(0, chips - 1)], all_recv.at[colour])
        remote(
            coeffs.at[colour, core], coeffs.at[colour, core], fwd_send, fwd_recv.at[colour], partner
        ).start()

    def place_of(colour):
        if direct:
            return out.at[:, colour, :, :, pl.ds(pl.multiple_of(me * piece, piece), piece)]
        return out.at[me, colour]

    relay(0)
    for colour in range(3):
        landed(coeffs.at[colour, 1 - core], fwd_recv.at[colour])
        table = jnp.stack([coeffs[colour, 0], coeffs[colour, 1]], axis=1).astype(F32)
        table = table.reshape(n * units, 8, nvec)[: NMOM * columns].reshape(NMOM, columns, 8, nvec)
        still = table[0]
        for i, (cosine, sine) in enumerate(turns):
            turned = table[len(plan) + i]
            still = still + cosine * turned + sine * swap_halves(turned)
        real_rows, imag_rows = [], []
        for slot in range(len(plan)):
            group = still if slot == 0 else table[slot]
            reals = jnp.concatenate([group[j, :4] for j in range(columns)])
            imags = jnp.concatenate([group[j, 4:] for j in range(columns)])
            real_rows += [reals, imags]
            imag_rows += [-imags, reals]
        lhs[0] = jnp.concatenate(real_rows).astype(BF16)
        lhs[1] = jnp.concatenate(imag_rows).astype(BF16)

        def rebuild(step, colour=colour):
            sites = pl.ds(pl.multiple_of(step * chunk, chunk), chunk)
            grid = jnp.dot(
                lhs[0], eig[0, colour, :, sites], preferred_element_type=F32
            ) + jnp.dot(lhs[1], eig[1, colour, :, sites], preferred_element_type=F32)
            grid = grid.reshape(len(plan), 2, base_rows // 2, chunk)
            real, imag = grid[0, 0], grid[0, 1]
            for slot in range(len(moving)):
                cosine = trig[2 * slot : 2 * slot + 1, sites]
                sine = trig[2 * slot + 1 : 2 * slot + 2, sites]
                real = real + cosine * grid[slot + 1, 0] - sine * grid[slot + 1, 1]
                imag = imag + cosine * grid[slot + 1, 1] + sine * grid[slot + 1, 0]
            source[: base_rows // 2, sites] = (real * scale_out).astype(BF16)
            source[base_rows // 2 :, sites] = (imag * scale_out).astype(BF16)

        each(0, steps, rebuild)
        if colour < 2:
            relay(colour + 1)

        def choose(peer_chip, colour=colour):
            chosen = jnp.dot(
                source[...], onehot[pl.ds(peer_chip, 1)][0], preferred_element_type=F32
            )
            for which in range(2):
                values = chosen[:, which * piece : (which + 1) * piece]
                staged[pl.ds(peer_chip * 2 + which, 1), colour] = values.reshape(
                    1, 2, columns, 4, piece
                ).astype(BF16)

        def send_pieces(other, colour=colour):
            choose(other)
            for which in range(2):
                peer = other * 2 + which
                remote(staged.at[peer, colour], place_of(colour), out_send, out_recv, peer).start()

        if colour < 2:
            far_chips(send_pieces)
            near_chips(send_pieces)
        else:
            near_chips(send_pieces)
            far_chips(send_pieces)
        choose(chip)
        remote(staged.at[partner, colour], place_of(colour), out_send, out_recv, partner).start()
        pltpu.make_async_copy(staged.at[me, colour], place_of(colour), own_sem).start()

    sent(from_core, core_send)
    sent(summed.at[:, pl.ds(0, chips - 1)], chip_send)
    sent(coeffs.at[:, 0, pl.ds(0, chips - 1)], all_send)
    sent(coeffs.at[:, 0], fwd_send)
    sent(wanted.at[pl.ds(0, n - 1)], index_send)
    pltpu.make_async_copy(staged.at[0], staged.at[0], own_sem).wait()
    sent(staged.at[pl.ds(0, n - 1)], out_send)
    landed(staged.at[pl.ds(0, n - 1)], out_recv)


def on_device(
    propagator, eigvecs, operator_weights, sink_time, term_index, term_sign, solver_order
):
    columns, length = propagator.shape[3:]
    nvec = eigvecs.shape[2]
    n = lax.axis_size("space")
    chips = n // 2
    piece = length // n
    units = -(-NMOM * columns // n)
    fixed = tuple(
        p for p in range(1, NMOM)
        if MOMENTA[p][:2] == (0, 0) and EXTENT * EXTENT % length == 0
    )
    moving = tuple(p for p in range(1, NMOM) if p not in fixed)
    assert fixed == tuple(range(len(moving) + 1, NMOM))
    rows = (1 + len(moving)) * columns * 8
    site_rows = columns * 8
    unit = (units, 8, nvec)
    direct = piece % 128 == 0
    out_shape = (2, 3, columns, 4, length) if direct else (n, 3, 2, columns, 4, piece)
    propagator = propagator.transpose(0, 1, 3, 2, 4)
    vmem = pl.BlockSpec(memory_space=pltpu.VMEM)
    smem = pl.BlockSpec(memory_space=pltpu.SMEM)
    hbm = pl.BlockSpec(memory_space=pl.ANY)
    dma = pltpu.SemaphoreType.DMA
    gathered = pl.pallas_call(
        functools.partial(
            kernel, n, units, columns, 1.0 / math.sqrt(3.0 * length * n),
            1.0 / math.sqrt(NMOM * nvec), 512, moving, fixed, direct,
        ),
        out_shape=jax.ShapeDtypeStruct(out_shape, BF16),
        in_specs=[hbm, hbm, smem, hbm, vmem, vmem, vmem],
        out_specs=hbm,
        scratch_shapes=[
            pltpu.VMEM(propagator.shape, BF16),
            pltpu.VMEM(eigvecs.shape, BF16),
            pltpu.VMEM(operator_weights.shape, F32),
            pltpu.VMEM((2 * len(moving), length), F32),
            pltpu.VMEM((rows, nvec), F32),
            pltpu.VMEM((3, chips, 2) + unit, F32),
            pltpu.VMEM((3, chips) + unit, F32),
            pltpu.VMEM((3, chips) + unit, BF16),
            pltpu.VMEM((3, chips) + unit, BF16),
            pltpu.VMEM((3, 2, chips) + unit, BF16),
            pltpu.VMEM((2, rows, nvec), BF16),
            pltpu.VMEM((site_rows, length), BF16),
            pltpu.VMEM((n, 1, piece), jnp.int32),
            pltpu.VMEM((chips, length, 2 * piece), BF16),
            pltpu.VMEM((n, 3, 2, columns, 4, piece), BF16),
            dma((7,)), dma((3,)), dma((3,)), dma((3,)), dma((3,)), dma((9,)),
        ],
        compiler_params=pltpu.CompilerParams(
            collective_id=0, has_side_effects=True, vmem_limit_bytes=60 * 2**20
        ),
    )(
        propagator, eigvecs, sink_time, operator_weights,
        term_index.T, term_sign.reshape(1, -1), solver_order.reshape(n, 1, piece),
    )
    if direct:
        return gathered.transpose(0, 1, 3, 2, 4)
    placed = gathered.transpose(2, 1, 4, 3, 0, 5)
    return placed.reshape(2, 3, 4, columns, length)


def solution(mesh):
    return jax.shard_map(
        on_device,
        mesh=mesh,
        in_specs=(
            P("grp", None, None, None, "space"),
            P("grp", None, None, "space"),
            P("grp", None, None),
            P("grp"),
            P(),
            P(),
            P("space"),
        ),
        out_specs=P("grp", None, None, None, "space"),
        check_vma=False,
    )
```

time: 60.6 us -> 58 us (0.957)
  Pallas kernels: 56.2 us -> 54.2 us
    unnamed x0 -> x1, local copies, waits for them, and re-layouts: none -> 2.93 us
    transpose x1 -> x0, local copies, waits for them, and re-layouts: 2.03 us -> none  [on_device(): gathered.reshape(n, 3, columns, 2, 4, piece).transpose(3, 1, 4, 2, 0, 5)]
    pallas_call x1, Pallas kernels: 56.2 us -> 54.2 us  [on_device(): pl.pallas_call(functools.partial(kernel, n, units, columns, 1.0 / math.sq...]
    reshape x1 -> x0, local copies, waits for them, and re-layouts: 1.17 us -> none  [on_device(): return placed.reshape(2, 3, 4, columns, length)]
where the time goes in v1:
time: 58 us; the launch traced here: 57.8 us
  Pallas kernels  54.2 us (93%)
  local copies, waits for them, and re-layouts  2.93 us (5%)
  between operations  0.66 us (1%)
    pallas_call x1, Pallas kernels, on_device(): pl.pallas_call(functools.partial(kernel, n, units, columns, 1.0 / math.sq...  54.2 us
    unnamed x1, local copies, waits for them, and re-layouts  2.93 us

profile of v1, /device:TPU:0, one launch (start us, length us, event | category | flops | bytes accessed | tf_op | source)
XLA Modules:
  0.0 57.8 jit_solution(9095106257518061459)
XLA Ops:
  0.7 54.2 %shard_map.73 = bf16[2,3,12,4,2048]{4,3,2,1,0:T(4,128)(2,1)} custom-call(bf16[2,3,12,4,2048]{4,3,2,1,0:T(4,128)(2,1)} %bitcast.6, bf16[2,3,256,2048]{3,2,1,0:T(8,128)(2,1)} %eig_hbm.1, s32[1]{0:T(128)S(6)} %copy.9.sink, f32[128,2,256]{2,1,0:T(2,128)} %table_hbm.1, s32[3,48]{1,0:T(4,128)} %bitcast.8, s32[1,48]{1,0:T(1,128)} %bitcast.9, s32[16,1,128]{2,1,0:T(1,128)} %bitcast.7), custom_call_target="tpu_custom_call" | custom-call | tf_op jit(solution)/shard_map/pallas_call | solution.py:388
  54.9 2.9 %copy.10 = bf16[2,3,4,12,2048]{4,2,3,1,0:T(4,128)(2,1)} copy(bf16[2,3,4,12,2048]{4,2,3,1,0:T(4,128)(2,1)} %bitcast.5) | data formatting | bytes 2359296

commit v2 on v1

v2 whole, which is shorter than its diff:
```python
import functools
import math

import jax
import jax.numpy as jnp
from jax import lax
from jax.experimental import pallas as pl
from jax.experimental.pallas import tpu as pltpu
from jax.sharding import PartitionSpec as P

NMOM = 4
EXTENT = 64
MOMENTA = ((0, 0, 0), (1, 0, 0), (0, 1, 0), (0, 0, 1))
F32 = jnp.float32
BF16 = jnp.bfloat16
MESH = pl.DeviceIdType.MESH


def swap_halves(x):
    top, bottom = x[..., :4, :], x[..., 4:, :]
    return jnp.concatenate([-bottom, top], axis=-2)


def dot_exact(a, b):
    high = b.astype(BF16)
    low = (b - high.astype(F32)).astype(BF16)
    return jnp.dot(a, high, preferred_element_type=F32) + jnp.dot(a, low, preferred_element_type=F32)


def kernel(
    n, groups, columns, scale_in, scale_out, chunk, moving, fixed, direct,
    prop_hbm, eig_hbm, sink, table_hbm, term_rows, term_sign, order, out,
    prop, eig, table_weights, trig, turn, acc, blocks, from_core, summed, from_chips, ready, coeffs,
    lhs, source, wanted, onehot, staged,
    load_sem, core_recv, chip_recv, all_recv, fwd_recv, sems,
):
    me = lax.axis_index("space")
    chips = n // 2
    half = chips // 2
    core = lax.rem(me, 2)
    chip = me // 2
    side = chip // half
    partner = me + 1 - 2 * core
    length = eig.shape[-1]
    nvec = eig.shape[2]
    piece = order.shape[-1]
    steps = length // chunk
    slots = 1 + len(moving)
    core_send, chip_send, all_send, fwd_send, index_send, index_recv, out_send, out_recv, own_sem = (
        sems.at[i] for i in range(9)
    )

    def each(lower, upper, body):
        def step(i, carry):
            body(i)
            return carry

        lax.fori_loop(lower, upper, step, 0)

    def far_chips(body):
        each(0, half, lambda t: body((1 - side) * half + lax.rem(chip + t, half)))

    def near_chips(body):
        each(1, half, lambda t: body(side * half + lax.rem(chip + t, half)))

    def remote(src, dst, send_sem, recv_sem, device):
        return pltpu.make_async_remote_copy(
            src_ref=src, dst_ref=dst, send_sem=send_sem, recv_sem=recv_sem,
            device_id={"space": device}, device_id_type=MESH,
        )

    def sent(ref, sem):
        remote(ref, ref, sem, sem, partner).wait_send()

    def landed(ref, sem):
        remote(ref, ref, sem, sem, partner).wait_recv()

    class Group:
        def __init__(self, index, start, depth):
            self.index, self.start, self.depth = index, start, depth
            self.first = 2 * start
            self.owners = 2 * depth
            self.left, self.width = 4 * start, 4 * depth
            below = chip - (half - start - depth)
            above = chip - (half + start)
            self.owns = ((below >= 0) & (below < depth)) | ((above >= 0) & (above < depth))
            self.mine = self.first + jnp.where(chip < half, below, depth + above)

        def chip_of(self, owner):
            return jnp.where(
                owner < self.depth, half - self.start - self.depth + owner,
                half + self.start + owner - self.depth,
            )

        def each_owner(self, body):
            def step(t):
                owner = lax.rem(t + (1 - side) * self.depth, self.owners)
                other = self.chip_of(owner)

                @pl.when(other != chip)
                def _():
                    body(self.first + owner, other)

            each(0, self.owners, step)

    plan, start = [], 0
    for index, depth in enumerate(groups):
        plan.append(Group(index, start, depth))
        start += depth

    loads = []
    for colour in range(3):
        loads.append((
            pltpu.make_async_copy(prop_hbm.at[:, colour], prop.at[:, colour], load_sem.at[colour]),
            pltpu.make_async_copy(eig_hbm.at[:, colour], eig.at[:, colour], load_sem.at[3 + colour]),
        ))

    def load(colour):
        for copy in loads[colour]:
            copy.start()

    load(0)
    barrier = pltpu.get_barrier_semaphore()
    each(1, n, lambda t: pl.semaphore_signal(
        barrier, inc=1, device_id={"space": lax.rem(me + t, n)}, device_id_type=MESH
    ))

    bits = EXTENT.bit_length() - 1
    low = EXTENT - 1

    def angles(p, site):
        coords = (site & low, (site >> bits) & low, site >> (2 * bits))
        winding = sum(step * coord for step, coord in zip(MOMENTA[p], coords) if step) & low
        return winding.astype(F32) * (2.0 * math.pi / EXTENT)

    tiles = length // 128
    compact = me * length + 128 * lax.broadcasted_iota(
        jnp.int32, (tiles, 128), 0
    ) + lax.broadcasted_iota(jnp.int32, (tiles, 128), 1)
    for slot, p in enumerate(moving):
        angle = angles(p, compact)
        for part, values in enumerate((jnp.cos(angle), jnp.sin(angle))):
            trig[2 * slot + part : 2 * slot + part + 1, :] = jnp.concatenate(
                [values[tile : tile + 1] for tile in range(tiles)], axis=1
            )
    for i, p in enumerate(fixed):
        angle = angles(p, 2 * length * lax.broadcasted_iota(jnp.int32, (chips, nvec), 0))
        turn[2 * i] = jnp.cos(angle)[:, None]
        turn[2 * i + 1] = jnp.sin(angle)[:, None]
    load(1)

    def core_copy(group, colour):
        owners = pl.ds(group.first, group.owners)
        return remote(
            blocks.at[colour, owners, 1 - core], from_core.at[colour, owners], core_send,
            core_recv.at[group.index, colour], partner,
        )

    def send_sums(group, colour):
        core_copy(group, colour).wait_recv()

        def send(owner, other):
            summed[colour, pl.ds(owner, 1)] = (
                blocks[colour, pl.ds(owner, 1), pl.ds(core, 1)][:, 0]
                + from_core[colour, pl.ds(owner, 1)]
            ).astype(BF16)
            remote(
                summed.at[colour, owner], from_chips.at[colour, chip], chip_send,
                chip_recv.at[colour], other * 2 + core,
            ).start()

        group.each_owner(send)

    def project(group, colour):
        rows = slots * group.width * 8
        acc[:rows] = jnp.zeros((rows, nvec), F32)
        picked = slice(group.left, group.left + group.width)

        def step(step):
            sites = pl.ds(pl.multiple_of(step * chunk, chunk), chunk)
            real = prop[0, colour, picked, :, sites].astype(F32)
            imag = prop[1, colour, picked, :, sites].astype(F32)
            straight = jnp.concatenate([real, imag], axis=1)
            crossed = jnp.concatenate([imag, -real], axis=1)
            first, second = [straight], [crossed]
            for slot in range(len(moving)):
                cosine = trig[2 * slot : 2 * slot + 1, sites][None]
                sine = trig[2 * slot + 1 : 2 * slot + 2, sites][None]
                first.append(cosine * straight + sine * crossed)
                second.append(cosine * crossed - sine * straight)
            first = jnp.concatenate(first).reshape(rows, chunk).astype(BF16)
            second = jnp.concatenate(second).reshape(rows, chunk).astype(BF16)
            dims = (((1,), (1,)), ((), ()))
            acc[:rows] += lax.dot_general(
                first, eig[0, colour, :, sites], dims, preferred_element_type=F32
            ) + lax.dot_general(
                second, eig[1, colour, :, sites], dims, preferred_element_type=F32
            )

        each(0, steps, step)
        made = (acc[:rows] * scale_in).reshape(slots, group.owners, 2, 8, nvec)
        for slot in range(slots):
            blocks[colour, group.first : group.first + group.owners, :, slot] = made[slot]

    pending = []
    for group in plan:
        for colour in range(3):
            if group.index == 0:
                for copy in loads[colour]:
                    copy.wait()
                if colour == 0:
                    load(2)
                    small_loads = (
                        pltpu.make_async_copy(table_hbm, table_weights, load_sem.at[6]),
                    )
                    for copy in small_loads:
                        copy.start()
            project(group, colour)
            if group.index == 0 and colour == 0:
                pl.semaphore_wait(barrier, n - 1)
            core_copy(group, colour).start()
            if group.index == 0 and colour == 0:

                def send_index(t):
                    peer = lax.rem(me + t, n)
                    remote(order.at[peer], wanted.at[me], index_send, index_recv, peer).start()

                each(1, n, send_index)
                wanted[pl.ds(me, 1)] = order[pl.ds(me, 1)]
            if pending:
                send_sums(*pending.pop())
            pending.append((group, colour))
    send_sums(*pending.pop())

    terms = term_rows.shape[1]
    for copy in small_loads:
        copy.wait()

    def contract(group):
        eye = lax.broadcasted_iota(jnp.int32, (terms, terms), 0) == lax.broadcasted_iota(
            jnp.int32, (terms, terms), 1
        )
        lane = lax.broadcasted_iota(jnp.int32, (terms, 24), 1)
        lane_channel = (4 * (lane >> 3) + (lane & 3)).astype(F32)
        lane_imag = (lane >> 2) & 1
        picks = []
        for which in range(2):
            row = term_rows[which : which + 1, :].astype(F32)
            column = jnp.sum(jnp.where(eye, row, 0.0), axis=1, keepdims=True)
            for part in range(2):
                hit = (lane_channel == column) & (lane_imag == part)
                picks.append(jnp.where(hit, 1.0, 0.0))
        picks = jnp.concatenate(picks).astype(BF16)
        sub = lax.broadcasted_iota(jnp.int32, (24, terms), 0)
        target = 4 * (sub >> 3) + (sub & 3) == term_rows[2:3, :]
        signs = (2 * term_sign[...] - 1).astype(F32)
        place_real = jnp.where(target & (((sub >> 2) & 1) == 0), signs, 0.0).astype(BF16)
        place_imag = jnp.where(target & (((sub >> 2) & 1) == 1), signs, 0.0).astype(BF16)
        weights = table_weights[sink[0, 0]]
        weight_real, weight_imag = weights[0:1, :], weights[1:2, :]

        totals = []
        for colour in range(3):
            own = blocks[colour, pl.ds(group.mine, 1), pl.ds(core, 1)][0, 0]
            own = own + from_core[colour, pl.ds(group.mine, 1)][0]
            landed(from_chips.at[colour, pl.ds(0, chips - 1)], chip_recv.at[colour])

            def turned(part, source_chip):
                kept = []
                for i in range(len(fixed)):
                    kept.append(turn[2 * i, pl.ds(source_chip, 1)][0] * part[0])
                    kept.append(turn[2 * i + 1, pl.ds(source_chip, 1)][0] * part[0])
                return kept

            def add_sum(t, carry, colour=colour):
                other = lax.rem(chip + chips - t, chips)
                part = from_chips[colour, pl.ds(other, 1)][0].astype(F32)
                return tuple(a + b for a, b in zip(carry, (part, *turned(part, other))))

            total, *kept = lax.fori_loop(1, chips, add_sum, (own, *turned(own, chip)))
            extra = [
                kept[2 * i] - swap_halves(kept[2 * i + 1]) for i in range(len(fixed))
            ]
            totals.append([total[slot] for slot in range(slots)] + extra)

        count = slots + len(fixed)
        block = jnp.concatenate([
            jnp.concatenate([total[unit] for total in totals]) for unit in range(count)
        ], axis=1)
        picked = dot_exact(picks, block)
        first_real, first_imag = picked[:terms], picked[terms : 2 * terms]
        other_real, other_imag = picked[2 * terms : 3 * terms], picked[3 * terms :]
        real_products, imag_products = [], []
        for unit in range(count):
            lanes = slice(unit * nvec, (unit + 1) * nvec)
            o_real, o_imag = other_real[:, lanes], other_imag[:, lanes]
            f_real, f_imag = first_real[:, lanes], first_imag[:, lanes]
            second_real = jnp.sum(
                weight_real * o_real - weight_imag * o_imag, axis=1, keepdims=True
            )
            second_imag = jnp.sum(
                weight_real * o_imag + weight_imag * o_real, axis=1, keepdims=True
            )
            real_products.append(f_real * second_real - f_imag * second_imag)
            imag_products.append(f_real * second_imag + f_imag * second_real)
        made = dot_exact(place_real, jnp.concatenate(real_products, axis=1)) + dot_exact(
            place_imag, jnp.concatenate(imag_products, axis=1)
        )
        acc[:24, :] = made[:, :nvec]
        for i in range(len(fixed)):
            acc[24 * (i + 1) : 24 * (i + 2), :] = made[:, (slots + i) * nvec : (slots + i + 1) * nvec]
        rest = made[:, nvec : slots * nvec].reshape(3, 8, (slots - 1) * nvec).astype(BF16)

        def merged(colour, other):
            value = acc[8 * colour : 8 * colour + 8, :]
            for i in range(len(fixed)):
                side_value = acc[24 * (i + 1) + 8 * colour : 24 * (i + 1) + 8 * colour + 8, :]
                value = value + turn[2 * i, pl.ds(other, 1)][0] * side_value
                value = value + turn[2 * i + 1, pl.ds(other, 1)][0] * swap_halves(side_value)
            return value.astype(BF16)

        for colour in range(3):
            others = [rest[colour, :, slot * nvec : (slot + 1) * nvec] for slot in range(slots - 1)]

            def send_coeffs(other, colour=colour, others=others):
                ready[colour, pl.ds(other, 1), 0] = merged(colour, other)[None]
                for slot in range(slots - 1):
                    ready[colour, pl.ds(other, 1), slot + 1] = others[slot][None]
                remote(
                    ready.at[colour, other], coeffs.at[colour, core, group.mine], all_send,
                    all_recv.at[group.index, colour], other * 2 + core,
                ).start()

            far_chips(send_coeffs)
            near_chips(send_coeffs)
            coeffs[colour, pl.ds(core, 1), pl.ds(group.mine, 1), 0] = merged(colour, chip)[None, None]
            for slot in range(slots - 1):
                coeffs[colour, pl.ds(core, 1), pl.ds(group.mine, 1), slot + 1] = others[slot][None, None]

    def build(peer_chip):
        position = lax.broadcasted_iota(jnp.int32, (length, piece), 0)
        for which in range(2):
            local = wanted[pl.ds(peer_chip * 2 + which, 1)][0] - me * length
            onehot[pl.ds(peer_chip, 1), :, which * piece : (which + 1) * piece] = jnp.where(
                position == local, 1.0, 0.0
            ).astype(BF16)[None]

    def build_all():
        landed(wanted.at[pl.ds(0, n - 1)], index_recv)
        each(0, chips, build)

    for i, group in enumerate(plan):
        if i == 0 and len(plan) == 1:
            build_all()
        pl.when(group.owns)(functools.partial(contract, group))
        if i == 0 and len(plan) > 1:
            build_all()

    def relay(group, colour):
        def take(count):
            landed(coeffs.at[colour, core, pl.ds(0, count)], all_recv.at[group.index, colour])

        pl.when(group.owns)(lambda: take(group.owners - 1))
        pl.when(jnp.logical_not(group.owns))(lambda: take(group.owners))
        owners = pl.ds(group.first, group.owners)
        remote(
            coeffs.at[colour, core, owners], coeffs.at[colour, core, owners], fwd_send,
            fwd_recv.at[group.index, colour], partner,
        ).start()

    def rebuild(group, colour):
        owners = pl.ds(group.first, group.owners)
        landed(coeffs.at[colour, 1 - core, owners], fwd_recv.at[group.index, colour])
        table = coeffs[colour, :, group.first : group.first + group.owners].astype(F32)
        real_rows, imag_rows = [], []
        for slot in range(slots):
            cells = [table[which, o, slot] for o in range(group.owners) for which in range(2)]
            reals = jnp.concatenate([cell[:4] for cell in cells])
            imags = jnp.concatenate([cell[4:] for cell in cells])
            real_rows += [reals, imags]
            imag_rows += [-imags, reals]
        quarter = 4 * group.width
        rows = slots * 2 * quarter
        lhs[0, :rows] = jnp.concatenate(real_rows).astype(BF16)
        lhs[1, :rows] = jnp.concatenate(imag_rows).astype(BF16)

        def step(step):
            sites = pl.ds(pl.multiple_of(step * chunk, chunk), chunk)
            grid = jnp.dot(
                lhs[0, :rows], eig[0, colour, :, sites], preferred_element_type=F32
            ) + jnp.dot(lhs[1, :rows], eig[1, colour, :, sites], preferred_element_type=F32)
            grid = grid.reshape(slots, 2, quarter, chunk)
            real, imag = grid[0, 0], grid[0, 1]
            for slot in range(len(moving)):
                cosine = trig[2 * slot : 2 * slot + 1, sites]
                sine = trig[2 * slot + 1 : 2 * slot + 2, sites]
                real = real + cosine * grid[slot + 1, 0] - sine * grid[slot + 1, 1]
                imag = imag + cosine * grid[slot + 1, 1] + sine * grid[slot + 1, 0]
            source[:quarter, sites] = (real * scale_out).astype(BF16)
            source[quarter : 2 * quarter, sites] = (imag * scale_out).astype(BF16)

        each(0, steps, step)

    def distribute(group, colour, last):
        picked = pl.ds(group.left, group.width)
        if direct:
            lanes = pl.ds(pl.multiple_of(me * piece, piece), piece)
            target = out.at[:, colour, picked, :, lanes]
        else:
            target = out.at[me, colour, :, picked]

        def choose(peer_chip):
            chosen = jnp.dot(
                source[: 8 * group.width], onehot[pl.ds(peer_chip, 1)][0], preferred_element_type=F32
            )
            for which in range(2):
                values = chosen[:, which * piece : (which + 1) * piece]
                staged[
                    pl.ds(peer_chip * 2 + which, 1), colour, :, group.left : group.left + group.width
                ] = values.reshape(1, 2, group.width, 4, piece).astype(BF16)

        def send_pieces(other):
            choose(other)
            for which in range(2):
                peer = other * 2 + which
                remote(staged.at[peer, colour, :, picked], target, out_send, out_recv, peer).start()

        if last:
            near_chips(send_pieces)
            far_chips(send_pieces)
        else:
            far_chips(send_pieces)
            near_chips(send_pieces)
        choose(chip)
        remote(staged.at[partner, colour, :, picked], target, out_send, out_recv, partner).start()
        pltpu.make_async_copy(staged.at[me, colour, :, picked], target, own_sem).start()

    work = [(group, colour) for group in plan for colour in range(3)]
    relay(*work[0])
    for i, (group, colour) in enumerate(work):
        rebuild(group, colour)
        if i + 1 < len(work):
            relay(*work[i + 1])
        distribute(group, colour, i + 1 == len(work))

    owns = functools.reduce(jnp.logical_or, [group.owns for group in plan])
    total_owners = 2 * sum(groups)

    def sent_sums(count):
        sent(summed.at[:, pl.ds(0, count)], chip_send)

    sent(from_core, core_send)

    @pl.when(owns)
    def _():
        sent_sums(total_owners - 1)
        sent(ready.at[:, pl.ds(0, chips - 1)], all_send)

    pl.when(jnp.logical_not(owns))(lambda: sent_sums(total_owners))
    sent(coeffs.at[:, 0], fwd_send)
    sent(wanted.at[pl.ds(0, n - 1)], index_send)
    pltpu.make_async_copy(staged.at[0], staged.at[0], own_sem).wait()
    sent(staged.at[pl.ds(0, n - 1)], out_send)
    landed(staged.at[pl.ds(0, n - 1)], out_recv)


def on_device(
    propagator, eigvecs, operator_weights, sink_time, term_index, term_sign, solver_order
):
    columns, length = propagator.shape[3:]
    nvec = eigvecs.shape[2]
    n = lax.axis_size("space")
    chips = n // 2
    piece = length // n
    groups = (columns // 4,)
    fixed = tuple(
        p for p in range(1, NMOM)
        if MOMENTA[p][:2] == (0, 0) and EXTENT * EXTENT % (2 * length) == 0
    )
    moving = tuple(p for p in range(1, NMOM) if p not in fixed)
    assert 4 * sum(groups) == columns and sum(groups) <= chips // 2
    slots = 1 + len(moving)
    owners = 2 * sum(groups)
    rows = slots * columns * 8
    site_rows = columns * 8
    cell = (slots, 8, nvec)
    direct = piece % 128 == 0
    out_shape = (2, 3, columns, 4, length) if direct else (n, 3, 2, columns, 4, piece)
    propagator = propagator.transpose(0, 1, 3, 2, 4)
    vmem = pl.BlockSpec(memory_space=pltpu.VMEM)
    hbm = pl.BlockSpec(memory_space=pltpu.HBM)
    dma = pltpu.SemaphoreType.DMA
    gathered = pl.pallas_call(
        functools.partial(
            kernel, n, groups, columns, 1.0 / math.sqrt(3.0 * length * n),
            1.0 / math.sqrt(NMOM * nvec), 512, moving, fixed, direct,
        ),
        out_shape=pltpu.VMEM(out_shape, BF16),
        in_specs=[hbm, hbm, pl.BlockSpec(memory_space=pltpu.SMEM), hbm, vmem, vmem, vmem],
        out_specs=pl.BlockSpec(memory_space=pl.ANY),
        scratch_shapes=[
            pltpu.VMEM(propagator.shape, BF16),
            pltpu.VMEM(eigvecs.shape, BF16),
            pltpu.VMEM(operator_weights.shape, F32),
            pltpu.VMEM((2 * len(moving), length), F32),
            pltpu.VMEM((2 * max(len(fixed), 1), chips, 1, nvec), F32),
            pltpu.VMEM((rows, nvec), F32),
            pltpu.VMEM((3, owners, 2) + cell, F32),
            pltpu.VMEM((3, owners) + cell, F32),
            pltpu.VMEM((3, owners) + cell, BF16),
            pltpu.VMEM((3, chips) + cell, BF16),
            pltpu.VMEM((3, chips) + cell, BF16),
            pltpu.VMEM((3, 2, owners) + cell, BF16),
            pltpu.VMEM((2, rows, nvec), BF16),
            pltpu.VMEM((site_rows, length), BF16),
            pltpu.VMEM((n, 1, piece), jnp.int32),
            pltpu.VMEM((chips, length, 2 * piece), BF16),
            pltpu.VMEM((n, 3, 2, columns, 4, piece), BF16),
            dma((8,)), dma((len(groups), 3)), dma((3,)), dma((len(groups), 3)), dma((len(groups), 3)),
            dma((9,)),
        ],
        compiler_params=pltpu.CompilerParams(
            collective_id=0, has_side_effects=True, vmem_limit_bytes=int(48 * 2**20)
        ),
    )(
        *(
            x if x.size == 1 else pltpu.with_memory_space_constraint(x, pltpu.HBM)
            for x in (
                propagator, eigvecs, sink_time.reshape(1, 1), operator_weights,
                term_index.T, term_sign.reshape(1, -1), solver_order.reshape(n, 1, piece),
            )
        )
    )
    if direct:
        return gathered.transpose(0, 1, 3, 2, 4)
    placed = gathered.transpose(2, 1, 4, 3, 0, 5)
    return placed.reshape(2, 3, 4, columns, length)


def solution(mesh):
    return jax.shard_map(
        on_device,
        mesh=mesh,
        in_specs=(
            P("grp", None, None, None, "space"),
            P("grp", None, None, "space"),
            P("grp", None, None),
            P("grp"),
            P(),
            P(),
            P("space"),
        ),
        out_specs=P("grp", None, None, None, "space"),
        check_vma=False,
    )
```

time: 58 us -> 54.1 us (0.933)
  local copies, waits for them, and re-layouts: 2.93 us -> 1.02 us
  Pallas kernels: 54.2 us -> 52.3 us
    pallas_call x1, Pallas kernels: 54.2 us -> 52.3 us  [on_device(): pl.pallas_call(functools.partial(kernel, n, groups, columns, 1.0 / math.s...]
    unnamed x1, local copies, waits for them, and re-layouts: 2.93 us -> 1.02 us
where the time goes in v2:
time: 54.1 us; the launch traced here: 53.9 us
  Pallas kernels  52.3 us (97%)
  local copies, waits for them, and re-layouts  1.02 us (2%)
  between operations  0.66 us (1%)
    pallas_call x1, Pallas kernels, on_device(): pl.pallas_call(functools.partial(kernel, n, groups, columns, 1.0 / math.s...  52.3 us

profile of v2, /device:TPU:0, one launch (start us, length us, event | category | flops | bytes accessed | tf_op | source)
XLA Modules:
  0.0 53.9 jit_solution(10370593599591548401)
XLA Ops:
  0.7 52.3 %shard_map.73 = bf16[2,3,12,4,2048]{4,3,2,1,0:T(4,128)(2,1)S(1)} custom-call(bf16[2,3,12,4,2048]{4,3,2,1,0:T(4,128)(2,1)} %bitcast.8, bf16[2,3,256,2048]{3,2,1,0:T(8,128)(2,1)} %eig_hbm.1, s32[1,1]{1,0:T(1,128)} %bitcast.6.sink, f32[128,2,256]{2,1,0:T(2,128)} %table_hbm.1, s32[3,48]{1,0:T(4,128)} %bitcast.10, s32[1,48]{1,0:T(1,128)} %bitcast.11, ...), custom_call_target="tpu_custom_call" | custom-call | tf_op jit(solution)/shard_map/pallas_call | solution.py:493
  52.9 1.0 %copy.9 = bf16[2,3,4,12,2048]{4,2,3,1,0:T(4,128)(2,1)} copy(bf16[2,3,4,12,2048]{4,2,3,1,0:T(4,128)(2,1)S(1)} %bitcast.7) | data formatting | bytes 2359296

commit v3 on v2

--- a/solution.py
+++ b/solution.py
@@ -29,8 +29,8 @@
 
 def kernel(
     n, groups, columns, scale_in, scale_out, chunk, moving, fixed, direct,
-    prop_hbm, eig_hbm, sink, table_hbm, term_rows, term_sign, order, out,
-    prop, eig, table_weights, trig, turn, acc, blocks, from_core, summed, from_chips, ready, coeffs,
+    prop_hbm, eig_hbm, sink, table_hbm, term_rows_hbm, term_sign_hbm, order_hbm, out,
+    prop, eig, table_weights, term_rows, term_sign, order, trig, turn, acc, blocks, from_core, summed, from_chips, ready, coeffs,
     lhs, source, wanted, onehot, staged,
     load_sem, core_recv, chip_recv, all_recv, fwd_recv, sems,
 ):
@@ -108,18 +108,38 @@
         plan.append(Group(index, start, depth))
         start += depth
 
-    loads = []
-    for colour in range(3):
-        loads.append((
-            pltpu.make_async_copy(prop_hbm.at[:, colour], prop.at[:, colour], load_sem.at[colour]),
-            pltpu.make_async_copy(eig_hbm.at[:, colour], eig.at[:, colour], load_sem.at[3 + colour]),
+    def load_of(colour, lower, upper, sem):
+        sites = slice(lower, upper)
+        return (
+            pltpu.make_async_copy(
+                prop_hbm.at[:, colour, :, :, sites], prop.at[:, colour, :, :, sites],
+                load_sem.at[sem],
+            ),
+            pltpu.make_async_copy(
+                eig_hbm.at[:, colour, :, sites], eig.at[:, colour, :, sites], load_sem.at[sem + 1]
+            ),
+        )
+
+    def start(copies):
+        for copy in copies:
+            copy.start()
+
+    def finish(copies):
+        for copy in copies:
+            copy.wait()
+
+    middle = length // 2
+    first_loads = (load_of(0, 0, middle, 0), load_of(0, middle, length, 2))
+    later_loads = (load_of(1, 0, length, 4), load_of(2, 0, length, 6))
+    small_loads = tuple(
+        pltpu.make_async_copy(remote_ref, own_ref, load_sem.at[8 + i])
+        for i, (remote_ref, own_ref) in enumerate((
+            (order_hbm, order), (table_hbm, table_weights), (term_rows_hbm, term_rows),
+            (term_sign_hbm, term_sign),
         ))
-
-    def load(colour):
-        for copy in loads[colour]:
-            copy.start()
-
-    load(0)
+    )
+    start(first_loads[0])
+    start(first_loads[1])
     barrier = pltpu.get_barrier_semaphore()
     each(1, n, lambda t: pl.semaphore_signal(
         barrier, inc=1, device_id={"space": lax.rem(me + t, n)}, device_id_type=MESH
@@ -147,7 +167,8 @@
         angle = angles(p, 2 * length * lax.broadcasted_iota(jnp.int32, (chips, nvec), 0))
         turn[2 * i] = jnp.cos(angle)[:, None]
         turn[2 * i + 1] = jnp.sin(angle)[:, None]
-    load(1)
+    start(small_loads)
+    start(later_loads[0])
 
     def core_copy(group, colour):
         owners = pl.ds(group.first, group.owners)
@@ -171,7 +192,7 @@
 
         group.each_owner(send)
 
-    def project(group, colour):
+    def project(group, colour, between=None):
         rows = slots * group.width * 8
         acc[:rows] = jnp.zeros((rows, nvec), F32)
         picked = slice(group.left, group.left + group.width)
@@ -197,7 +218,12 @@
                 second, eig[1, colour, :, sites], dims, preferred_element_type=F32
             )
 
-        each(0, steps, step)
+        if between is None:
+            each(0, steps, step)
+        else:
+            each(0, steps // 2, step)
+            between()
+            each(steps // 2, steps, step)
         made = (acc[:rows] * scale_in).reshape(slots, group.owners, 2, 8, nvec)
         for slot in range(slots):
             blocks[colour, group.first : group.first + group.owners, :, slot] = made[slot]
@@ -205,21 +231,20 @@
     pending = []
     for group in plan:
         for colour in range(3):
-            if group.index == 0:
-                for copy in loads[colour]:
-                    copy.wait()
-                if colour == 0:
-                    load(2)
-                    small_loads = (
-                        pltpu.make_async_copy(table_hbm, table_weights, load_sem.at[6]),
-                    )
-                    for copy in small_loads:
-                        copy.start()
-            project(group, colour)
+            if group.index > 0:
+                project(group, colour)
+            elif colour == 0:
+                finish(first_loads[0])
+                start(later_loads[1])
+                project(group, colour, lambda: finish(first_loads[1]))
+            else:
+                finish(later_loads[colour - 1])
+                project(group, colour)
             if group.index == 0 and colour == 0:
                 pl.semaphore_wait(barrier, n - 1)
             core_copy(group, colour).start()
             if group.index == 0 and colour == 0:
+                finish(small_loads[:1])
 
                 def send_index(t):
                     peer = lax.rem(me + t, n)
@@ -233,8 +258,7 @@
     send_sums(*pending.pop())
 
     terms = term_rows.shape[1]
-    for copy in small_loads:
-        copy.wait()
+    finish(small_loads[1:])
 
     def contract(group):
         eye = lax.broadcasted_iota(jnp.int32, (terms, terms), 0) == lax.broadcasted_iota(
@@ -368,7 +392,7 @@
             fwd_recv.at[group.index, colour], partner,
         ).start()
 
-    def rebuild(group, colour):
+    def rebuild(group, colour, place):
         owners = pl.ds(group.first, group.owners)
         landed(coeffs.at[colour, 1 - core, owners], fwd_recv.at[group.index, colour])
         table = coeffs[colour, :, group.first : group.first + group.owners].astype(F32)
@@ -396,34 +420,43 @@
                 sine = trig[2 * slot + 1 : 2 * slot + 2, sites]
                 real = real + cosine * grid[slot + 1, 0] - sine * grid[slot + 1, 1]
                 imag = imag + cosine * grid[slot + 1, 1] + sine * grid[slot + 1, 0]
-            source[:quarter, sites] = (real * scale_out).astype(BF16)
-            source[quarter : 2 * quarter, sites] = (imag * scale_out).astype(BF16)
+            base = 2 * quarter * place
+            source[base : base + quarter, sites] = (real * scale_out).astype(BF16)
+            source[base + quarter : base + 2 * quarter, sites] = (imag * scale_out).astype(BF16)
 
         each(0, steps, step)
 
-    def distribute(group, colour, last):
+    def distribute(group, colours, last):
         picked = pl.ds(group.left, group.width)
+        taken = pl.ds(colours[0], len(colours))
         if direct:
             lanes = pl.ds(pl.multiple_of(me * piece, piece), piece)
-            target = out.at[:, colour, picked, :, lanes]
+            target = out.at[:, taken, picked, :, lanes]
         else:
-            target = out.at[me, colour, :, picked]
+            target = out.at[me, :, taken, picked]
 
         def choose(peer_chip):
             chosen = jnp.dot(
-                source[: 8 * group.width], onehot[pl.ds(peer_chip, 1)][0], preferred_element_type=F32
+                source[: 8 * group.width * len(colours)], onehot[pl.ds(peer_chip, 1)][0],
+                preferred_element_type=F32,
             )
             for which in range(2):
-                values = chosen[:, which * piece : (which + 1) * piece]
-                staged[
-                    pl.ds(peer_chip * 2 + which, 1), colour, :, group.left : group.left + group.width
-                ] = values.reshape(1, 2, group.width, 4, piece).astype(BF16)
+                values = chosen[:, which * piece : (which + 1) * piece].reshape(
+                    len(colours), 2, group.width, 4, piece
+                ).astype(BF16)
+                for i, colour in enumerate(colours):
+                    staged[
+                        pl.ds(peer_chip * 2 + which, 1), :, colour,
+                        group.left : group.left + group.width,
+                    ] = values[i : i + 1]
 
         def send_pieces(other):
             choose(other)
             for which in range(2):
                 peer = other * 2 + which
-                remote(staged.at[peer, colour, :, picked], target, out_send, out_recv, peer).start()
+                remote(
+                    staged.at[peer, :, taken, picked], target, out_send, out_recv, peer
+                ).start()
 
         if last:
             near_chips(send_pieces)
@@ -432,16 +465,20 @@
             far_chips(send_pieces)
             near_chips(send_pieces)
         choose(chip)
-        remote(staged.at[partner, colour, :, picked], target, out_send, out_recv, partner).start()
-        pltpu.make_async_copy(staged.at[me, colour, :, picked], target, own_sem).start()
-
-    work = [(group, colour) for group in plan for colour in range(3)]
+        remote(staged.at[partner, :, taken, picked], target, out_send, out_recv, partner).start()
+        pltpu.make_async_copy(staged.at[me, :, taken, picked], target, own_sem).start()
+
+    batches = [(0, (0,)), (0, (1, 2))] + [(index, (0, 1, 2)) for index in range(1, len(plan))]
+    batches = [(plan[index], colours) for index, colours in batches]
+    work = [(group, colour) for group, colours in batches for colour in colours]
     relay(*work[0])
-    for i, (group, colour) in enumerate(work):
-        rebuild(group, colour)
-        if i + 1 < len(work):
-            relay(*work[i + 1])
-        distribute(group, colour, i + 1 == len(work))
+    for batch, (group, colours) in enumerate(batches):
+        for place, colour in enumerate(colours):
+            rebuild(group, colour, place)
+            done = work.index((group, colour)) + 1
+            if done < len(work):
+                relay(*work[done])
+        distribute(group, colours, batch + 1 == len(batches))
 
     owns = functools.reduce(jnp.logical_or, [group.owns for group in plan])
     total_owners = 2 * sum(groups)
@@ -472,7 +509,7 @@
     n = lax.axis_size("space")
     chips = n // 2
     piece = length // n
-    groups = (columns // 4,)
+    groups = (columns // 4 - 1, 1)
     fixed = tuple(
         p for p in range(1, NMOM)
         if MOMENTA[p][:2] == (0, 0) and EXTENT * EXTENT % (2 * length) == 0
@@ -485,9 +522,9 @@
     site_rows = columns * 8
     cell = (slots, 8, nvec)
     direct = piece % 128 == 0
-    out_shape = (2, 3, columns, 4, length) if direct else (n, 3, 2, columns, 4, piece)
+    out_shape = (2, 3, columns, 4, length) if direct else (n, 2, 3, columns, 4, piece)
     propagator = propagator.transpose(0, 1, 3, 2, 4)
-    vmem = pl.BlockSpec(memory_space=pltpu.VMEM)
+    smem = pl.BlockSpec(memory_space=pltpu.SMEM)
     hbm = pl.BlockSpec(memory_space=pltpu.HBM)
     dma = pltpu.SemaphoreType.DMA
     gathered = pl.pallas_call(
@@ -496,12 +533,15 @@
             1.0 / math.sqrt(NMOM * nvec), 512, moving, fixed, direct,
         ),
         out_shape=pltpu.VMEM(out_shape, BF16),
-        in_specs=[hbm, hbm, pl.BlockSpec(memory_space=pltpu.SMEM), hbm, vmem, vmem, vmem],
+        in_specs=[hbm, hbm, smem, hbm, hbm, hbm, hbm],
         out_specs=pl.BlockSpec(memory_space=pl.ANY),
         scratch_shapes=[
             pltpu.VMEM(propagator.shape, BF16),
             pltpu.VMEM(eigvecs.shape, BF16),
             pltpu.VMEM(operator_weights.shape, F32),
+            pltpu.VMEM(term_index.shape[::-1], jnp.int32),
+            pltpu.VMEM((1,) + term_sign.shape, jnp.int32),
+            pltpu.VMEM((n, 1, piece), jnp.int32),
             pltpu.VMEM((2 * len(moving), length), F32),
             pltpu.VMEM((2 * max(len(fixed), 1), chips, 1, nvec), F32),
             pltpu.VMEM((rows, nvec), F32),
@@ -512,11 +552,11 @@
             pltpu.VMEM((3, chips) + cell, BF16),
             pltpu.VMEM((3, 2, owners) + cell, BF16),
             pltpu.VMEM((2, rows, nvec), BF16),
-            pltpu.VMEM((site_rows, length), BF16),
+            pltpu.VMEM((2 * site_rows, length), BF16),
             pltpu.VMEM((n, 1, piece), jnp.int32),
             pltpu.VMEM((chips, length, 2 * piece), BF16),
-            pltpu.VMEM((n, 3, 2, columns, 4, piece), BF16),
-            dma((8,)), dma((len(groups), 3)), dma((3,)), dma((len(groups), 3)), dma((len(groups), 3)),
+            pltpu.VMEM((n, 2, 3, columns, 4, piece), BF16),
+            dma((12,)), dma((len(groups), 3)), dma((3,)), dma((len(groups), 3)), dma((len(groups), 3)),
             dma((9,)),
         ],
         compiler_params=pltpu.CompilerParams(
@@ -533,7 +573,7 @@
     )
     if direct:
         return gathered.transpose(0, 1, 3, 2, 4)
-    placed = gathered.transpose(2, 1, 4, 3, 0, 5)
+    placed = gathered.transpose(1, 2, 4, 3, 0, 5)
     return placed.reshape(2, 3, 4, columns, length)
 
 

time: 54.1 us -> 51.3 us (0.948)
  Pallas kernels: 52.3 us -> 49.5 us
    pallas_call x1, Pallas kernels: 52.3 us -> 49.5 us  [on_device(): pl.pallas_call(functools.partial(kernel, n, groups, columns, 1.0 / math.s...]
where the time goes in v3:
time: 51.3 us; the launch traced here: 51.2 us
  Pallas kernels  49.5 us (96%)
  local copies, waits for them, and re-layouts  1.02 us (2%)
  between operations  0.66 us (1%)
    pallas_call x1, Pallas kernels, on_device(): pl.pallas_call(functools.partial(kernel, n, groups, columns, 1.0 / math.s...  49.5 us

profile of v3, /device:TPU:0, one launch (start us, length us, event | category | flops | bytes accessed | tf_op | source)
XLA Modules:
  0.0 51.2 jit_solution(4339223810612003169)
XLA Ops:
  0.7 49.5 %shard_map.73 = bf16[2,3,12,4,2048]{4,3,2,1,0:T(4,128)(2,1)S(1)} custom-call(bf16[2,3,12,4,2048]{4,3,2,1,0:T(4,128)(2,1)} %bitcast.8, bf16[2,3,256,2048]{3,2,1,0:T(8,128)(2,1)} %eig_hbm.1, s32[1,1]{1,0:T(1,128)} %bitcast.6.sink, f32[128,2,256]{2,1,0:T(2,128)} %table_hbm.1, s32[3,48]{1,0:T(4,128)} %bitcast.10, s32[1,48]{1,0:T(1,128)} %bitcast.11, ...), custom_call_target="tpu_custom_call" | custom-call | tf_op jit(solution)/shard_map/pallas_call | solution.py:530
  50.2 1.0 %copy.9 = bf16[2,3,4,12,2048]{4,2,3,1,0:T(4,128)(2,1)} copy(bf16[2,3,4,12,2048]{4,2,3,1,0:T(4,128)(2,1)S(1)} %bitcast.7) | data formatting | bytes 2359296

commit v4 on v3

--- a/solution.py
+++ b/solution.py
@@ -108,8 +108,11 @@
         plan.append(Group(index, start, depth))
         start += depth
 
-    def load_of(colour, lower, upper, sem):
-        sites = slice(lower, upper)
+    middle = length // 2
+
+    def load(colour, part):
+        sites = slice(part * middle, (part + 1) * middle)
+        sem = 4 * colour + 2 * part
         return (
             pltpu.make_async_copy(
                 prop_hbm.at[:, colour, :, :, sites], prop.at[:, colour, :, :, sites],
@@ -128,18 +131,15 @@
         for copy in copies:
             copy.wait()
 
-    middle = length // 2
-    first_loads = (load_of(0, 0, middle, 0), load_of(0, middle, length, 2))
-    later_loads = (load_of(1, 0, length, 4), load_of(2, 0, length, 6))
     small_loads = tuple(
-        pltpu.make_async_copy(remote_ref, own_ref, load_sem.at[8 + i])
+        pltpu.make_async_copy(remote_ref, own_ref, load_sem.at[12 + i])
         for i, (remote_ref, own_ref) in enumerate((
             (order_hbm, order), (table_hbm, table_weights), (term_rows_hbm, term_rows),
             (term_sign_hbm, term_sign),
         ))
     )
-    start(first_loads[0])
-    start(first_loads[1])
+    start(load(0, 0))
+    start(load(0, 1))
     barrier = pltpu.get_barrier_semaphore()
     each(1, n, lambda t: pl.semaphore_signal(
         barrier, inc=1, device_id={"space": lax.rem(me + t, n)}, device_id_type=MESH
@@ -168,12 +168,13 @@
         turn[2 * i] = jnp.cos(angle)[:, None]
         turn[2 * i + 1] = jnp.sin(angle)[:, None]
     start(small_loads)
-    start(later_loads[0])
+    start(load(1, 0))
+    start(load(1, 1))
 
     def core_copy(group, colour):
         owners = pl.ds(group.first, group.owners)
         return remote(
-            blocks.at[colour, owners, 1 - core], from_core.at[colour, owners], core_send,
+            blocks.at[colour, 1 - core, owners], from_core.at[colour, owners], core_send,
             core_recv.at[group.index, colour], partner,
         )
 
@@ -181,9 +182,8 @@
         core_copy(group, colour).wait_recv()
 
         def send(owner, other):
-            summed[colour, pl.ds(owner, 1)] = (
-                blocks[colour, pl.ds(owner, 1), pl.ds(core, 1)][:, 0]
-                + from_core[colour, pl.ds(owner, 1)]
+            summed[colour, owner] = (
+                blocks[colour, core, owner] + from_core[colour, owner]
             ).astype(BF16)
             remote(
                 summed.at[colour, owner], from_chips.at[colour, chip], chip_send,
@@ -192,70 +192,73 @@
 
         group.each_owner(send)
 
-    def project(group, colour, between=None):
-        rows = slots * group.width * 8
-        acc[:rows] = jnp.zeros((rows, nvec), F32)
+    def project(group, colour, between):
+        quarter = slots * 4 * group.width
+        wide = -(-quarter // 128) * 128
         picked = slice(group.left, group.left + group.width)
-
-        def step(step):
-            sites = pl.ds(pl.multiple_of(step * chunk, chunk), chunk)
-            real = prop[0, colour, picked, :, sites].astype(F32)
-            imag = prop[1, colour, picked, :, sites].astype(F32)
-            straight = jnp.concatenate([real, imag], axis=1)
-            crossed = jnp.concatenate([imag, -real], axis=1)
-            first, second = [straight], [crossed]
+        total = None
+        for part in range(2):
+            between(part)
+            sites = slice(part * middle, (part + 1) * middle)
+            real = prop[0, colour, picked, :, sites].astype(F32).reshape(4 * group.width, middle)
+            imag = prop[1, colour, picked, :, sites].astype(F32).reshape(4 * group.width, middle)
+            reals, imags = [real], [imag]
             for slot in range(len(moving)):
-                cosine = trig[2 * slot : 2 * slot + 1, sites][None]
-                sine = trig[2 * slot + 1 : 2 * slot + 2, sites][None]
-                first.append(cosine * straight + sine * crossed)
-                second.append(cosine * crossed - sine * straight)
-            first = jnp.concatenate(first).reshape(rows, chunk).astype(BF16)
-            second = jnp.concatenate(second).reshape(rows, chunk).astype(BF16)
-            dims = (((1,), (1,)), ((), ()))
-            acc[:rows] += lax.dot_general(
-                first, eig[0, colour, :, sites], dims, preferred_element_type=F32
-            ) + lax.dot_general(
-                second, eig[1, colour, :, sites], dims, preferred_element_type=F32
-            )
-
-        if between is None:
-            each(0, steps, step)
-        else:
-            each(0, steps // 2, step)
-            between()
-            each(steps // 2, steps, step)
-        made = (acc[:rows] * scale_in).reshape(slots, group.owners, 2, 8, nvec)
+                cosine = trig[2 * slot : 2 * slot + 1, sites]
+                sine = trig[2 * slot + 1 : 2 * slot + 2, sites]
+                reals.append(cosine * real + sine * imag)
+                imags.append(cosine * imag - sine * real)
+            spare = [jnp.zeros((wide - quarter, middle), F32)] if wide > quarter else []
+            rows = jnp.concatenate(reals + spare + imags + spare).astype(BF16)
+            both = jnp.concatenate([eig[0, colour, :, sites], eig[1, colour, :, sites]])
+            made = lax.dot_general(
+                both, rows, (((1,), (1,)), ((), ())), preferred_element_type=F32
+            )
+            total = made if total is None else total + made
+        with_real, with_imag = total[:nvec] * scale_in, total[nvec:] * scale_in
+        real = (with_real[:, :wide] + with_imag[:, wide:]).T[:quarter]
+        imag = (with_real[:, wide:] - with_imag[:, :wide]).T[:quarter]
+        shape = (slots, 2, group.owners, 4, nvec)
+        made = jnp.concatenate([real.reshape(shape), imag.reshape(shape)], axis=3)
         for slot in range(slots):
-            blocks[colour, group.first : group.first + group.owners, :, slot] = made[slot]
-
-    pending = []
+            blocks[colour, :, group.first : group.first + group.owners, slot] = made[slot]
+
+    def send_index(t):
+        peer = lax.rem(me + t, n)
+        remote(order.at[peer], wanted.at[me], index_send, index_recv, peer).start()
+
     for group in plan:
-        for colour in range(3):
-            if group.index > 0:
-                project(group, colour)
-            elif colour == 0:
-                finish(first_loads[0])
-                start(later_loads[1])
-                project(group, colour, lambda: finish(first_loads[1]))
-            else:
-                finish(later_loads[colour - 1])
-                project(group, colour)
-            if group.index == 0 and colour == 0:
-                pl.semaphore_wait(barrier, n - 1)
+        opening = group.index == 0
+
+        def stage(colour, group=group, opening=opening):
+            def between(part):
+                if opening:
+                    finish(load(colour, part))
+                    if part == 0:
+
+                        @pl.when(colour == 0)
+                        def _():
+                            start(load(2, 0))
+                            start(load(2, 1))
+
+            project(group, colour, between)
+            if opening:
+                pl.when(colour == 0)(lambda: pl.semaphore_wait(barrier, n - 1))
             core_copy(group, colour).start()
-            if group.index == 0 and colour == 0:
-                finish(small_loads[:1])
-
-                def send_index(t):
-                    peer = lax.rem(me + t, n)
-                    remote(order.at[peer], wanted.at[me], index_send, index_recv, peer).start()
-
-                each(1, n, send_index)
-                wanted[pl.ds(me, 1)] = order[pl.ds(me, 1)]
-            if pending:
-                send_sums(*pending.pop())
-            pending.append((group, colour))
-    send_sums(*pending.pop())
+
+            @pl.when(colour == 0)
+            def _():
+                if opening:
+                    finish(small_loads[:1])
+                    each(1, n, send_index)
+                    wanted[pl.ds(me, 1)] = order[pl.ds(me, 1)]
+                else:
+                    send_sums(plan[group.index - 1], 2)
+
+            pl.when(colour > 0)(lambda: send_sums(group, colour - 1))
+
+        each(0, 3, stage)
+    send_sums(plan[-1], 2)
 
     terms = term_rows.shape[1]
     finish(small_loads[1:])
@@ -285,8 +288,7 @@
 
         totals = []
         for colour in range(3):
-            own = blocks[colour, pl.ds(group.mine, 1), pl.ds(core, 1)][0, 0]
-            own = own + from_core[colour, pl.ds(group.mine, 1)][0]
+            own = blocks[colour, core, group.mine] + from_core[colour, group.mine]
             landed(from_chips.at[colour, pl.ds(0, chips - 1)], chip_recv.at[colour])
 
             def turned(part, source_chip):
@@ -393,92 +395,89 @@
         ).start()
 
     def rebuild(group, colour, place):
-        owners = pl.ds(group.first, group.owners)
-        landed(coeffs.at[colour, 1 - core, owners], fwd_recv.at[group.index, colour])
-        table = coeffs[colour, :, group.first : group.first + group.owners].astype(F32)
-        real_rows, imag_rows = [], []
-        for slot in range(slots):
-            cells = [table[which, o, slot] for o in range(group.owners) for which in range(2)]
-            reals = jnp.concatenate([cell[:4] for cell in cells])
-            imags = jnp.concatenate([cell[4:] for cell in cells])
-            real_rows += [reals, imags]
-            imag_rows += [-imags, reals]
-        quarter = 4 * group.width
-        rows = slots * 2 * quarter
-        lhs[0, :rows] = jnp.concatenate(real_rows).astype(BF16)
-        lhs[1, :rows] = jnp.concatenate(imag_rows).astype(BF16)
+        landed(
+            coeffs.at[colour, 1 - core, pl.ds(group.first, group.owners)],
+            fwd_recv.at[group.index, colour],
+        )
+        height = group.width * slots * 8
+        lhs[:height] = coeffs[colour, :, group.first : group.first + group.owners].reshape(
+            height, nvec
+        )
+        base = pl.multiple_of(place * 8 * group.width, 8 * group.width)
 
         def step(step):
             sites = pl.ds(pl.multiple_of(step * chunk, chunk), chunk)
-            grid = jnp.dot(
-                lhs[0, :rows], eig[0, colour, :, sites], preferred_element_type=F32
-            ) + jnp.dot(lhs[1, :rows], eig[1, colour, :, sites], preferred_element_type=F32)
-            grid = grid.reshape(slots, 2, quarter, chunk)
-            real, imag = grid[0, 0], grid[0, 1]
+            x, y = (
+                jnp.dot(
+                    lhs[:height], eig[part, colour, :, sites], preferred_element_type=F32
+                ).reshape(group.width, slots, 8, chunk)
+                for part in range(2)
+            )
+            straight, crossed = x[:, 0], y[:, 0]
             for slot in range(len(moving)):
-                cosine = trig[2 * slot : 2 * slot + 1, sites]
-                sine = trig[2 * slot + 1 : 2 * slot + 2, sites]
-                real = real + cosine * grid[slot + 1, 0] - sine * grid[slot + 1, 1]
-                imag = imag + cosine * grid[slot + 1, 1] + sine * grid[slot + 1, 0]
-            base = 2 * quarter * place
-            source[base : base + quarter, sites] = (real * scale_out).astype(BF16)
-            source[base + quarter : base + 2 * quarter, sites] = (imag * scale_out).astype(BF16)
+                cosine = trig[2 * slot : 2 * slot + 1, sites][None]
+                sine = trig[2 * slot + 1 : 2 * slot + 2, sites][None]
+                straight = straight + cosine * x[:, slot + 1] - sine * y[:, slot + 1]
+                crossed = crossed + cosine * y[:, slot + 1] + sine * x[:, slot + 1]
+            made = (straight + swap_halves(crossed)) * scale_out
+            source[pl.ds(base, 8 * group.width), sites] = made.reshape(
+                8 * group.width, chunk
+            ).astype(BF16)
 
         each(0, steps, step)
 
     def distribute(group, colours, last):
         picked = pl.ds(group.left, group.width)
         taken = pl.ds(colours[0], len(colours))
+        height = 8 * group.width * len(colours)
         if direct:
             lanes = pl.ds(pl.multiple_of(me * piece, piece), piece)
             target = out.at[:, taken, picked, :, lanes]
         else:
             target = out.at[me, :, taken, picked]
 
-        def choose(peer_chip):
-            chosen = jnp.dot(
-                source[: 8 * group.width * len(colours)], onehot[pl.ds(peer_chip, 1)][0],
-                preferred_element_type=F32,
-            )
+        def send_pieces(t):
+            if last:
+                near = (t < half - 1) | (t == chips - 1)
+                step = jnp.where(t == chips - 1, 0, t + 1)
+            else:
+                near, step = t >= half, t + 1
+            other = jnp.where(near, side, 1 - side) * half + lax.rem(chip + step, half)
+            chosen = jnp.dot(source[:height], onehot[other], preferred_element_type=F32)
+            chosen = chosen.reshape(len(colours), group.width, 8, 2 * piece)
             for which in range(2):
-                values = chosen[:, which * piece : (which + 1) * piece].reshape(
-                    len(colours), 2, group.width, 4, piece
-                ).astype(BF16)
+                values = chosen[..., which * piece : (which + 1) * piece]
                 for i, colour in enumerate(colours):
-                    staged[
-                        pl.ds(peer_chip * 2 + which, 1), :, colour,
-                        group.left : group.left + group.width,
-                    ] = values[i : i + 1]
-
-        def send_pieces(other):
-            choose(other)
-            for which in range(2):
-                peer = other * 2 + which
+                    for part in range(2):
+                        staged[
+                            2 * other + which, part, colour, group.left : group.left + group.width
+                        ] = values[i, :, 4 * part : 4 * part + 4].astype(BF16)
+
+            def send(peer):
                 remote(
                     staged.at[peer, :, taken, picked], target, out_send, out_recv, peer
                 ).start()
 
-        if last:
-            near_chips(send_pieces)
-            far_chips(send_pieces)
-        else:
-            far_chips(send_pieces)
-            near_chips(send_pieces)
-        choose(chip)
-        remote(staged.at[partner, :, taken, picked], target, out_send, out_recv, partner).start()
-        pltpu.make_async_copy(staged.at[me, :, taken, picked], target, own_sem).start()
-
-    batches = [(0, (0,)), (0, (1, 2))] + [(index, (0, 1, 2)) for index in range(1, len(plan))]
-    batches = [(plan[index], colours) for index, colours in batches]
-    work = [(group, colour) for group, colours in batches for colour in colours]
-    relay(*work[0])
-    for batch, (group, colours) in enumerate(batches):
-        for place, colour in enumerate(colours):
-            rebuild(group, colour, place)
-            done = work.index((group, colour)) + 1
-            if done < len(work):
-                relay(*work[done])
-        distribute(group, colours, batch + 1 == len(batches))
+            @pl.when(other != chip)
+            def _():
+                send(2 * other)
+                send(2 * other + 1)
+
+            @pl.when(other == chip)
+            def _():
+                send(partner)
+                pltpu.make_async_copy(staged.at[me, :, taken, picked], target, own_sem).start()
+
+        each(0, chips, send_pieces)
+
+    batches = [(plan[0], (0,)), (plan[0], (1, 2))] + [(group, (0, 1, 2)) for group in plan[1:]]
+    relay(plan[0], 0)
+    for i, (group, colours) in enumerate(batches):
+        each(colours[0], colours[-1] + 1, lambda colour: rebuild(group, colour, colour - colours[0]))
+        if i + 1 < len(batches):
+            following, later = batches[i + 1]
+            each(later[0], later[-1] + 1, lambda colour: relay(following, colour))
+        distribute(group, colours, i + 1 == len(batches))
 
     owns = functools.reduce(jnp.logical_or, [group.owns for group in plan])
     total_owners = 2 * sum(groups)
@@ -509,7 +508,7 @@
     n = lax.axis_size("space")
     chips = n // 2
     piece = length // n
-    groups = (columns // 4 - 1, 1)
+    groups = (2,) * (columns // 8) + (1,) * (columns % 8 // 4)
     fixed = tuple(
         p for p in range(1, NMOM)
         if MOMENTA[p][:2] == (0, 0) and EXTENT * EXTENT % (2 * length) == 0
@@ -544,19 +543,19 @@
             pltpu.VMEM((n, 1, piece), jnp.int32),
             pltpu.VMEM((2 * len(moving), length), F32),
             pltpu.VMEM((2 * max(len(fixed), 1), chips, 1, nvec), F32),
-            pltpu.VMEM((rows, nvec), F32),
-            pltpu.VMEM((3, owners, 2) + cell, F32),
+            pltpu.VMEM((24 * (1 + len(fixed)), nvec), F32),
+            pltpu.VMEM((3, 2, owners) + cell, F32),
             pltpu.VMEM((3, owners) + cell, F32),
             pltpu.VMEM((3, owners) + cell, BF16),
             pltpu.VMEM((3, chips) + cell, BF16),
             pltpu.VMEM((3, chips) + cell, BF16),
             pltpu.VMEM((3, 2, owners) + cell, BF16),
-            pltpu.VMEM((2, rows, nvec), BF16),
+            pltpu.VMEM((rows, nvec), BF16),
             pltpu.VMEM((2 * site_rows, length), BF16),
             pltpu.VMEM((n, 1, piece), jnp.int32),
             pltpu.VMEM((chips, length, 2 * piece), BF16),
             pltpu.VMEM((n, 2, 3, columns, 4, piece), BF16),
-            dma((12,)), dma((len(groups), 3)), dma((3,)), dma((len(groups), 3)), dma((len(groups), 3)),
+            dma((16,)), dma((len(groups), 3)), dma((3,)), dma((len(groups), 3)), dma((len(groups), 3)),
             dma((9,)),
         ],
         compiler_params=pltpu.CompilerParams(

time: 51.3 us -> 50.2 us (0.979)
  Pallas kernels: 49.5 us -> 48.3 us
    pallas_call x1, Pallas kernels: 49.5 us -> 48.3 us  [on_device(): pl.pallas_call(functools.partial(kernel, n, groups, columns, 1.0 / math.s...]
where the time goes in v4:
time: 50.2 us; the launch traced here: 50 us
  Pallas kernels  48.3 us (96%)
  local copies, waits for them, and re-layouts  1.02 us (2%)
  between operations  0.66 us (1%)
    pallas_call x1, Pallas kernels, on_device(): pl.pallas_call(functools.partial(kernel, n, groups, columns, 1.0 / math.s...  48.3 us
    unnamed x1, local copies, waits for them, and re-layouts  1.02 us

profile of v4, /device:TPU:0, one launch (start us, length us, event | category | flops | bytes accessed | tf_op | source)
XLA Modules:
  0.0 50.0 jit_solution(13437567761701184558)
XLA Ops:
  0.7 48.3 %shard_map.73 = bf16[2,3,12,4,2048]{4,3,2,1,0:T(4,128)(2,1)S(1)} custom-call(bf16[2,3,12,4,2048]{4,3,2,1,0:T(4,128)(2,1)} %bitcast.8, bf16[2,3,256,2048]{3,2,1,0:T(8,128)(2,1)} %eig_hbm.1, s32[1,1]{1,0:T(1,128)} %bitcast.6.sink, f32[128,2,256]{2,1,0:T(2,128)} %table_hbm.1, s32[3,48]{1,0:T(4,128)} %bitcast.10, s32[1,48]{1,0:T(1,128)} %bitcast.11, ...), custom_call_target="tpu_custom_call" | custom-call | tf_op jit(solution)/shard_map/pallas_call | solution.py:529
  49.0 1.0 %copy.9 = bf16[2,3,4,12,2048]{4,2,3,1,0:T(4,128)(2,1)} copy(bf16[2,3,4,12,2048]{4,2,3,1,0:T(4,128)(2,1)S(1)} %bitcast.7) | data formatting | bytes 2359296

commit v5 on v4

--- a/solution.py
+++ b/solution.py
@@ -30,9 +30,9 @@
 def kernel(
     n, groups, columns, scale_in, scale_out, chunk, moving, fixed, direct,
     prop_hbm, eig_hbm, sink, table_hbm, term_rows_hbm, term_sign_hbm, order_hbm, out,
-    prop, eig, table_weights, term_rows, term_sign, order, trig, turn, acc, blocks, from_core, summed, from_chips, ready, coeffs,
+    prop, eig, table_weights, term_rows, term_sign, order, trig, turn, acc, blocks, from_core, summed, from_chips, ready, coeffs, rest,
     lhs, source, wanted, onehot, staged,
-    load_sem, core_recv, chip_recv, all_recv, fwd_recv, sems,
+    load_sem, core_recv, chip_recv, all_recv, fwd_recv, mate_recv, sems,
 ):
     me = lax.axis_index("space")
     chips = n // 2
@@ -46,9 +46,10 @@
     piece = order.shape[-1]
     steps = length // chunk
     slots = 1 + len(moving)
-    core_send, chip_send, all_send, fwd_send, index_send, index_recv, out_send, out_recv, own_sem = (
-        sems.at[i] for i in range(9)
-    )
+    (
+        core_send, chip_send, all_send, fwd_send, pass_send, partner_send, index_send, index_recv,
+        out_send, out_recv, own_sem,
+    ) = (sems.at[i] for i in range(11))
 
     def each(lower, upper, body):
         def step(i, carry):
@@ -85,6 +86,12 @@
             above = chip - (half + start)
             self.owns = ((below >= 0) & (below < depth)) | ((above >= 0) & (above < depth))
             self.mine = self.first + jnp.where(chip < half, below, depth + above)
+            place = self.mine - self.first
+            self.seat = core * self.owners + place
+            self.mate_chip = jnp.where(place < depth, half + place, half - 2 * depth + place)
+            self.passes = (chip >= half - depth) & (chip < half + depth)
+            mate = jnp.where(chip < half, chip - half + 2 * depth, chip - half)
+            self.mate_seat = core * self.owners + mate
 
         def chip_of(self, owner):
             return jnp.where(
@@ -262,6 +269,22 @@
 
     terms = term_rows.shape[1]
     finish(small_loads[1:])
+
+    def spread(cell, arrived, sem, last_sem):
+        def send(other):
+            for which in range(2):
+                remote(cell, cell, sem, arrived, other * 2 + which).start()
+
+        near_chips(send)
+        remote(cell, cell, last_sem, arrived, partner).start()
+
+    def pass_on(group):
+        def step(colour):
+            cell = rest.at[colour, group.mate_seat]
+            landed(cell, mate_recv.at[colour])
+            spread(cell, all_recv.at[group.index, colour], pass_send, partner_send)
+
+        each(0, 3, step)
 
     def contract(group):
         eye = lax.broadcasted_iota(jnp.int32, (terms, terms), 0) == lax.broadcasted_iota(
@@ -332,36 +355,52 @@
         made = dot_exact(place_real, jnp.concatenate(real_products, axis=1)) + dot_exact(
             place_imag, jnp.concatenate(imag_products, axis=1)
         )
+        if group.index > 0:
+            for unit in range(count):
+                part = made[:, unit * nvec : (unit + 1) * nvec].reshape(3, 8, nvec).astype(BF16)
+                for colour in range(3):
+                    rest[colour, group.seat, unit] = part[colour]
+
+            def send_rest(colour):
+                cell = rest.at[colour, group.seat]
+                remote(
+                    cell, cell, all_send, mate_recv.at[colour], group.mate_chip * 2 + core
+                ).start()
+                spread(cell, all_recv.at[group.index, colour], all_send, all_send)
+
+            each(0, 3, send_rest)
+            return
         acc[:24, :] = made[:, :nvec]
         for i in range(len(fixed)):
             acc[24 * (i + 1) : 24 * (i + 2), :] = made[:, (slots + i) * nvec : (slots + i + 1) * nvec]
-        rest = made[:, nvec : slots * nvec].reshape(3, 8, (slots - 1) * nvec).astype(BF16)
+        plain = made[:, nvec : slots * nvec].reshape(3, 8, (slots - 1) * nvec).astype(BF16)
 
         def merged(colour, other):
             value = acc[8 * colour : 8 * colour + 8, :]
             for i in range(len(fixed)):
                 side_value = acc[24 * (i + 1) + 8 * colour : 24 * (i + 1) + 8 * colour + 8, :]
-                value = value + turn[2 * i, pl.ds(other, 1)][0] * side_value
-                value = value + turn[2 * i + 1, pl.ds(other, 1)][0] * swap_halves(side_value)
+                value = value + turn[2 * i, other] * side_value
+                value = value + turn[2 * i + 1, other] * swap_halves(side_value)
             return value.astype(BF16)
 
         for colour in range(3):
-            others = [rest[colour, :, slot * nvec : (slot + 1) * nvec] for slot in range(slots - 1)]
-
-            def send_coeffs(other, colour=colour, others=others):
-                ready[colour, pl.ds(other, 1), 0] = merged(colour, other)[None]
+            others = [plain[colour, :, slot * nvec : (slot + 1) * nvec] for slot in range(slots - 1)]
+            target = coeffs.at[colour, core, group.mine]
+            coeffs[colour, core, group.mine, 0] = merged(colour, chip)
+            for slot in range(slots - 1):
+                coeffs[colour, core, group.mine, slot + 1] = others[slot]
+
+            def send_coeffs(other, colour=colour, others=others, target=target):
+                ready[colour, other, 0] = merged(colour, other)
                 for slot in range(slots - 1):
-                    ready[colour, pl.ds(other, 1), slot + 1] = others[slot][None]
+                    ready[colour, other, slot + 1] = others[slot]
                 remote(
-                    ready.at[colour, other], coeffs.at[colour, core, group.mine], all_send,
-                    all_recv.at[group.index, colour], other * 2 + core,
+                    ready.at[colour, other], target, all_send, all_recv.at[group.index, colour],
+                    other * 2 + core,
                 ).start()
 
             far_chips(send_coeffs)
             near_chips(send_coeffs)
-            coeffs[colour, pl.ds(core, 1), pl.ds(group.mine, 1), 0] = merged(colour, chip)[None, None]
-            for slot in range(slots - 1):
-                coeffs[colour, pl.ds(core, 1), pl.ds(group.mine, 1), slot + 1] = others[slot][None, None]
 
     def build(peer_chip):
         position = lax.broadcasted_iota(jnp.int32, (length, piece), 0)
@@ -382,34 +421,48 @@
         if i == 0 and len(plan) > 1:
             build_all()
 
-    def relay(group, colour):
+    def relay(colour):
+        group = plan[0]
+
         def take(count):
-            landed(coeffs.at[colour, core, pl.ds(0, count)], all_recv.at[group.index, colour])
+            landed(coeffs.at[colour, core, pl.ds(0, count)], all_recv.at[0, colour])
 
         pl.when(group.owns)(lambda: take(group.owners - 1))
         pl.when(jnp.logical_not(group.owns))(lambda: take(group.owners))
-        owners = pl.ds(group.first, group.owners)
-        remote(
-            coeffs.at[colour, core, owners], coeffs.at[colour, core, owners], fwd_send,
-            fwd_recv.at[group.index, colour], partner,
-        ).start()
-
-    def rebuild(group, colour, place):
-        landed(
-            coeffs.at[colour, 1 - core, pl.ds(group.first, group.owners)],
-            fwd_recv.at[group.index, colour],
-        )
+        cells = coeffs.at[colour, core]
+        remote(cells, cells, fwd_send, fwd_recv.at[colour], partner).start()
+
+    def rebuild(group, colour):
         height = group.width * slots * 8
-        lhs[:height] = coeffs[colour, :, group.first : group.first + group.owners].reshape(
-            height, nvec
-        )
-        base = pl.multiple_of(place * 8 * group.width, 8 * group.width)
+        if group.index == 0:
+            landed(coeffs.at[colour, 1 - core], fwd_recv.at[colour])
+            lhs[: group.width] = coeffs[colour].reshape(group.width, slots, 8, nvec)
+        else:
+            for passes in range(2):
+                for owns in range(2):
+
+                    @pl.when((group.passes == (passes == 1)) & (group.owns == (owns == 1)))
+                    def _(count=2 * group.owners - passes - owns):
+                        landed(
+                            rest.at[colour, pl.ds(0, count)], all_recv.at[group.index, colour]
+                        )
+
+            table = rest[colour].reshape(group.width, slots + len(fixed), 8, nvec)
+            still = table[:, 0].astype(F32)
+            for i in range(len(fixed)):
+                turned = table[:, slots + i].astype(F32)
+                still = still + turn[2 * i, chip] * turned
+                still = still + turn[2 * i + 1, chip] * swap_halves(turned)
+            lhs[: group.width, 0] = still.astype(BF16)
+            lhs[: group.width, 1:] = table[:, 1:slots]
+        base = pl.multiple_of(colour * 8 * group.width, 8 * group.width)
 
         def step(step):
             sites = pl.ds(pl.multiple_of(step * chunk, chunk), chunk)
             x, y = (
                 jnp.dot(
-                    lhs[:height], eig[part, colour, :, sites], preferred_element_type=F32
+                    lhs[: group.width].reshape(height, nvec), eig[part, colour, :, sites],
+                    preferred_element_type=F32,
                 ).reshape(group.width, slots, 8, chunk)
                 for part in range(2)
             )
@@ -426,10 +479,11 @@
 
         each(0, steps, step)
 
-    def distribute(group, colours, last):
+    def distribute(group, colours, far):
         picked = pl.ds(group.left, group.width)
         taken = pl.ds(colours[0], len(colours))
         height = 8 * group.width * len(colours)
+        base = 8 * group.width * colours[0]
         if direct:
             lanes = pl.ds(pl.multiple_of(me * piece, piece), piece)
             target = out.at[:, taken, picked, :, lanes]
@@ -437,13 +491,10 @@
             target = out.at[me, :, taken, picked]
 
         def send_pieces(t):
-            if last:
-                near = (t < half - 1) | (t == chips - 1)
-                step = jnp.where(t == chips - 1, 0, t + 1)
-            else:
-                near, step = t >= half, t + 1
-            other = jnp.where(near, side, 1 - side) * half + lax.rem(chip + step, half)
-            chosen = jnp.dot(source[:height], onehot[other], preferred_element_type=F32)
+            other = (1 - side if far else side) * half + lax.rem(chip + t, half)
+            chosen = jnp.dot(
+                source[base : base + height], onehot[other], preferred_element_type=F32
+            )
             chosen = chosen.reshape(len(colours), group.width, 8, 2 * piece)
             for which in range(2):
                 values = chosen[..., which * piece : (which + 1) * piece]
@@ -458,26 +509,38 @@
                     staged.at[peer, :, taken, picked], target, out_send, out_recv, peer
                 ).start()
 
-            @pl.when(other != chip)
-            def _():
+            if far:
                 send(2 * other)
                 send(2 * other + 1)
-
-            @pl.when(other == chip)
-            def _():
-                send(partner)
-                pltpu.make_async_copy(staged.at[me, :, taken, picked], target, own_sem).start()
-
-        each(0, chips, send_pieces)
-
-    batches = [(plan[0], (0,)), (plan[0], (1, 2))] + [(group, (0, 1, 2)) for group in plan[1:]]
-    relay(plan[0], 0)
-    for i, (group, colours) in enumerate(batches):
-        each(colours[0], colours[-1] + 1, lambda colour: rebuild(group, colour, colour - colours[0]))
-        if i + 1 < len(batches):
-            following, later = batches[i + 1]
-            each(later[0], later[-1] + 1, lambda colour: relay(following, colour))
-        distribute(group, colours, i + 1 == len(batches))
+            else:
+
+                @pl.when(other != chip)
+                def _():
+                    send(2 * other)
+                    send(2 * other + 1)
+
+                @pl.when(other == chip)
+                def _():
+                    send(partner)
+                    pltpu.make_async_copy(
+                        staged.at[me, :, taken, picked], target, own_sem
+                    ).start()
+
+        each(0 if far else 1, half if far else half + 1, send_pieces)
+
+    relay(0)
+    rebuild(plan[0], 0)
+    distribute(plan[0], (0,), True)
+    each(1, 3, relay)
+    pl.when(plan[1].passes)(functools.partial(pass_on, plan[1]))
+    each(1, 3, lambda colour: rebuild(plan[0], colour))
+    distribute(plan[0], (1, 2), True)
+    distribute(plan[0], (0, 1, 2), False)
+    rebuild(plan[1], 0)
+    distribute(plan[1], (0,), True)
+    each(1, 3, lambda colour: rebuild(plan[1], colour))
+    distribute(plan[1], (0, 1, 2), False)
+    distribute(plan[1], (1, 2), True)
 
     owns = functools.reduce(jnp.logical_or, [group.owns for group in plan])
     total_owners = 2 * sum(groups)
@@ -487,12 +550,24 @@
 
     sent(from_core, core_send)
 
-    @pl.when(owns)
+    pl.when(owns)(lambda: sent_sums(total_owners - 1))
+    pl.when(jnp.logical_not(owns))(lambda: sent_sums(total_owners))
+
+    line = 8 * (slots + len(fixed)) * nvec // length
+
+    @pl.when(plan[0].owns)
     def _():
-        sent_sums(total_owners - 1)
         sent(ready.at[:, pl.ds(0, chips - 1)], all_send)
 
-    pl.when(jnp.logical_not(owns))(lambda: sent_sums(total_owners))
+    @pl.when(plan[1].owns)
+    def _():
+        sent(eig.at[0, :, pl.ds(0, 2 * half * line)], all_send)
+
+    @pl.when(plan[1].passes)
+    def _():
+        sent(eig.at[0, :, pl.ds(0, 2 * (half - 1) * line)], pass_send)
+        sent(rest.at[:, 0], partner_send)
+
     sent(coeffs.at[:, 0], fwd_send)
     sent(wanted.at[pl.ds(0, n - 1)], index_send)
     pltpu.make_async_copy(staged.at[0], staged.at[0], own_sem).wait()
@@ -508,7 +583,7 @@
     n = lax.axis_size("space")
     chips = n // 2
     piece = length // n
-    groups = (2,) * (columns // 8) + (1,) * (columns % 8 // 4)
+    groups = (1,) * (columns % 8 // 4) + (2,) * (columns // 8)
     fixed = tuple(
         p for p in range(1, NMOM)
         if MOMENTA[p][:2] == (0, 0) and EXTENT * EXTENT % (2 * length) == 0
@@ -517,8 +592,7 @@
     assert 4 * sum(groups) == columns and sum(groups) <= chips // 2
     slots = 1 + len(moving)
     owners = 2 * sum(groups)
-    rows = slots * columns * 8
-    site_rows = columns * 8
+    assert len(groups) == 2 and 8 * (slots + len(fixed)) * nvec % length == 0
     cell = (slots, 8, nvec)
     direct = piece % 128 == 0
     out_shape = (2, 3, columns, 4, length) if direct else (n, 2, 3, columns, 4, piece)
@@ -529,7 +603,7 @@
     gathered = pl.pallas_call(
         functools.partial(
             kernel, n, groups, columns, 1.0 / math.sqrt(3.0 * length * n),
-            1.0 / math.sqrt(NMOM * nvec), 512, moving, fixed, direct,
+            1.0 / math.sqrt(NMOM * nvec), length, moving, fixed, direct,
         ),
         out_shape=pltpu.VMEM(out_shape, BF16),
         in_specs=[hbm, hbm, smem, hbm, hbm, hbm, hbm],
@@ -549,14 +623,15 @@
             pltpu.VMEM((3, owners) + cell, BF16),
             pltpu.VMEM((3, chips) + cell, BF16),
             pltpu.VMEM((3, chips) + cell, BF16),
-            pltpu.VMEM((3, 2, owners) + cell, BF16),
-            pltpu.VMEM((rows, nvec), BF16),
-            pltpu.VMEM((2 * site_rows, length), BF16),
+            pltpu.VMEM((3, 2, 2 * groups[0]) + cell, BF16),
+            pltpu.VMEM((3, 4 * groups[1], slots + len(fixed), 8, nvec), BF16),
+            pltpu.VMEM((4 * max(groups), slots, 8, nvec), BF16),
+            pltpu.VMEM((12 * 8 * max(groups), length), BF16),
             pltpu.VMEM((n, 1, piece), jnp.int32),
             pltpu.VMEM((chips, length, 2 * piece), BF16),
             pltpu.VMEM((n, 2, 3, columns, 4, piece), BF16),
-            dma((16,)), dma((len(groups), 3)), dma((3,)), dma((len(groups), 3)), dma((len(groups), 3)),
-            dma((9,)),
+            dma((16,)), dma((len(groups), 3)), dma((3,)), dma((len(groups), 3)), dma((3,)), dma((3,)),
+            dma((11,)),
         ],
         compiler_params=pltpu.CompilerParams(
             collective_id=0, has_side_effects=True, vmem_limit_bytes=int(48 * 2**20)

time: 50.2 us -> 48.4 us (0.964)
  Pallas kernels: 48.3 us -> 46.5 us
    pallas_call x1, Pallas kernels: 48.3 us -> 46.5 us  [on_device(): pl.pallas_call(functools.partial(kernel, n, groups, columns, 1.0 / math.s...]
where the time goes in v5:
time: 48.4 us; the launch traced here: 48.2 us
  Pallas kernels  46.5 us (96%)
  local copies, waits for them, and re-layouts  1.02 us (2%)
  between operations  0.66 us (1%)
    pallas_call x1, Pallas kernels, on_device(): pl.pallas_call(functools.partial(kernel, n, groups, columns, 1.0 / math.s...  46.5 us
    unnamed x1, local copies, waits for them, and re-layouts  1.02 us

profile of v5, /device:TPU:0, one launch (start us, length us, event | category | flops | bytes accessed | tf_op | source)
XLA Modules:
  0.0 48.2 jit_solution(15925711740451757136)
XLA Ops:
  0.7 46.5 %shard_map.73 = bf16[2,3,12,4,2048]{4,3,2,1,0:T(4,128)(2,1)S(1)} custom-call(bf16[2,3,12,4,2048]{4,3,2,1,0:T(4,128)(2,1)} %bitcast.8, bf16[2,3,256,2048]{3,2,1,0:T(8,128)(2,1)} %eig_hbm.1, s32[1,1]{1,0:T(1,128)} %bitcast.6.sink, f32[128,2,256]{2,1,0:T(2,128)} %table_hbm.1, s32[3,48]{1,0:T(4,128)} %bitcast.10, s32[1,48]{1,0:T(1,128)} %bitcast.11, ...), custom_call_target="tpu_custom_call" | custom-call | tf_op jit(solution)/shard_map/pallas_call | solution.py:603
  47.2 1.0 %copy.9 = bf16[2,3,4,12,2048]{4,2,3,1,0:T(4,128)(2,1)} copy(bf16[2,3,4,12,2048]{4,2,3,1,0:T(4,128)(2,1)S(1)} %bitcast.7) | data formatting | bytes 2359296

commit v6 on v5

--- a/solution.py
+++ b/solution.py
@@ -28,11 +28,12 @@
 
 
 def kernel(
-    n, groups, columns, scale_in, scale_out, chunk, moving, fixed, direct,
+    n, depth, columns, scale_in, scale_out, chunk, moving, fixed, direct,
     prop_hbm, eig_hbm, sink, table_hbm, term_rows_hbm, term_sign_hbm, order_hbm, out,
-    prop, eig, table_weights, term_rows, term_sign, order, trig, turn, acc, blocks, from_core, summed, from_chips, ready, coeffs, rest,
-    lhs, source, wanted, onehot, staged,
-    load_sem, core_recv, chip_recv, all_recv, fwd_recv, mate_recv, sems,
+    prop, eig, table_weights, term_rows, term_sign, order, trig, turn, acc,
+    blocks_a, blocks_b, from_core_a, from_core_b, summed_a, summed_b, from_chips_a, from_chips_b,
+    ready, coeffs, rest, lhs, source, wanted, onehot, staged,
+    load_sem, core_recv, chip_recv, all_recv, fwd_recv, mate_recv, pass_send, sems,
 ):
     me = lax.axis_index("space")
     chips = n // 2
@@ -47,9 +48,9 @@
     steps = length // chunk
     slots = 1 + len(moving)
     (
-        core_send, chip_send, all_send, fwd_send, pass_send, partner_send, index_send, index_recv,
-        out_send, out_recv, own_sem,
-    ) = (sems.at[i] for i in range(11))
+        core_send_a, core_send_b, chip_send_a, chip_send_b, all_send_a, all_send_b, fwd_send_a,
+        fwd_send_b, index_send, index_recv, out_send, out_recv, own_sem,
+    ) = (sems.at[i] for i in range(13))
 
     def each(lower, upper, body):
         def step(i, carry):
@@ -76,44 +77,39 @@
     def landed(ref, sem):
         remote(ref, ref, sem, sem, partner).wait_recv()
 
+    owners = 2 * depth
+    central = (chip >= half - depth) & (chip < half + depth)
+    place = chip - half + depth
+
+    def each_owner(body):
+        def step(t):
+            owner = lax.rem(t + (1 - side) * depth, owners)
+            other = half - depth + owner
+
+            @pl.when(other != chip)
+            def _():
+                body(owner, other)
+
+        each(0, owners, step)
+
     class Group:
-        def __init__(self, index, start, depth):
-            self.index, self.start, self.depth = index, start, depth
-            self.first = 2 * start
-            self.owners = 2 * depth
-            self.left, self.width = 4 * start, 4 * depth
-            below = chip - (half - start - depth)
-            above = chip - (half + start)
-            self.owns = ((below >= 0) & (below < depth)) | ((above >= 0) & (above < depth))
-            self.mine = self.first + jnp.where(chip < half, below, depth + above)
-            place = self.mine - self.first
-            self.seat = core * self.owners + place
-            self.mate_chip = jnp.where(place < depth, half + place, half - 2 * depth + place)
-            self.passes = (chip >= half - depth) & (chip < half + depth)
-            mate = jnp.where(chip < half, chip - half + 2 * depth, chip - half)
-            self.mate_seat = core * self.owners + mate
-
-        def chip_of(self, owner):
-            return jnp.where(
-                owner < self.depth, half - self.start - self.depth + owner,
-                half + self.start + owner - self.depth,
-            )
-
-        def each_owner(self, body):
-            def step(t):
-                owner = lax.rem(t + (1 - side) * self.depth, self.owners)
-                other = self.chip_of(owner)
-
-                @pl.when(other != chip)
-                def _():
-                    body(self.first + owner, other)
-
-            each(0, self.owners, step)
-
-    plan, start = [], 0
-    for index, depth in enumerate(groups):
-        plan.append(Group(index, start, depth))
-        start += depth
+        def __init__(self, index, left, cores, *refs):
+            self.index, self.left, self.cores = index, left, cores
+            self.width = owners * len(cores)
+            self.owns = central & (core == 1) if len(cores) == 1 else central
+            self.row = core if len(cores) == 2 else 0
+            self.blocks, self.from_core, self.summed, self.from_chips = refs[:4]
+            self.core_send, self.chip_send = refs[4:]
+
+    plan = (
+        Group(
+            0, 0, (1,), blocks_a, from_core_a, summed_a, from_chips_a, core_send_a, chip_send_a
+        ),
+        Group(
+            1, owners, (0, 1), blocks_b, from_core_b, summed_b, from_chips_b, core_send_b,
+            chip_send_b,
+        ),
+    )
 
     middle = length // 2
 
@@ -179,25 +175,37 @@
     start(load(1, 1))
 
     def core_copy(group, colour):
-        owners = pl.ds(group.first, group.owners)
+        row = 1 - core if len(group.cores) == 2 else 0
         return remote(
-            blocks.at[colour, 1 - core, owners], from_core.at[colour, owners], core_send,
+            group.blocks.at[colour, row], group.from_core.at[colour], group.core_send,
             core_recv.at[group.index, colour], partner,
         )
 
+    def exchange(group, colour):
+        if len(group.cores) == 2:
+            core_copy(group, colour).start()
+        else:
+            pl.when(core == 0)(lambda: core_copy(group, colour).start())
+
     def send_sums(group, colour):
-        core_copy(group, colour).wait_recv()
-
-        def send(owner, other):
-            summed[colour, owner] = (
-                blocks[colour, core, owner] + from_core[colour, owner]
-            ).astype(BF16)
-            remote(
-                summed.at[colour, owner], from_chips.at[colour, chip], chip_send,
-                chip_recv.at[colour], other * 2 + core,
-            ).start()
-
-        group.each_owner(send)
+        def run():
+            core_copy(group, colour).wait_recv()
+
+            def send(owner, other):
+                group.summed[colour, owner] = (
+                    group.blocks[colour, group.row, owner] + group.from_core[colour, owner]
+                ).astype(BF16)
+                remote(
+                    group.summed.at[colour, owner], group.from_chips.at[colour, chip],
+                    group.chip_send, chip_recv.at[group.index, colour], other * 2 + core,
+                ).start()
+
+            each_owner(send)
+
+        if len(group.cores) == 2:
+            run()
+        else:
+            pl.when(core == 1)(run)
 
     def project(group, colour, between):
         quarter = slots * 4 * group.width
@@ -225,10 +233,10 @@
         with_real, with_imag = total[:nvec] * scale_in, total[nvec:] * scale_in
         real = (with_real[:, :wide] + with_imag[:, wide:]).T[:quarter]
         imag = (with_real[:, wide:] - with_imag[:, :wide]).T[:quarter]
-        shape = (slots, 2, group.owners, 4, nvec)
+        shape = (slots, len(group.cores), owners, 4, nvec)
         made = jnp.concatenate([real.reshape(shape), imag.reshape(shape)], axis=3)
         for slot in range(slots):
-            blocks[colour, :, group.first : group.first + group.owners, slot] = made[slot]
+            group.blocks[colour, :, :, slot] = made[slot]
 
     def send_index(t):
         peer = lax.rem(me + t, n)
@@ -251,7 +259,7 @@
             project(group, colour, between)
             if opening:
                 pl.when(colour == 0)(lambda: pl.semaphore_wait(barrier, n - 1))
-            core_copy(group, colour).start()
+            exchange(group, colour)
 
             @pl.when(colour == 0)
             def _():
@@ -270,21 +278,17 @@
     terms = term_rows.shape[1]
     finish(small_loads[1:])
 
-    def spread(cell, arrived, sem, last_sem):
-        def send(other):
-            for which in range(2):
-                remote(cell, cell, sem, arrived, other * 2 + which).start()
-
-        near_chips(send)
-        remote(cell, cell, last_sem, arrived, partner).start()
-
-    def pass_on(group):
-        def step(colour):
-            cell = rest.at[colour, group.mate_seat]
-            landed(cell, mate_recv.at[colour])
-            spread(cell, all_recv.at[group.index, colour], pass_send, partner_send)
-
-        each(0, 3, step)
+    def spread(cell, colour, sem):
+        near_chips(
+            lambda other: remote(
+                cell, cell, sem, all_recv.at[1, colour], other * 2 + core
+            ).start()
+        )
+
+    def pass_on(colour):
+        cell = rest.at[colour, core * owners + lax.rem(place + depth, owners)]
+        landed(cell, mate_recv.at[colour])
+        spread(cell, colour, pass_send.at[colour])
 
     def contract(group):
         eye = lax.broadcasted_iota(jnp.int32, (terms, terms), 0) == lax.broadcasted_iota(
@@ -311,8 +315,10 @@
 
         totals = []
         for colour in range(3):
-            own = blocks[colour, core, group.mine] + from_core[colour, group.mine]
-            landed(from_chips.at[colour, pl.ds(0, chips - 1)], chip_recv.at[colour])
+            own = group.blocks[colour, group.row, place] + group.from_core[colour, place]
+            landed(
+                group.from_chips.at[colour, pl.ds(0, chips - 1)], chip_recv.at[group.index, colour]
+            )
 
             def turned(part, source_chip):
                 kept = []
@@ -323,7 +329,7 @@
 
             def add_sum(t, carry, colour=colour):
                 other = lax.rem(chip + chips - t, chips)
-                part = from_chips[colour, pl.ds(other, 1)][0].astype(F32)
+                part = group.from_chips[colour, other].astype(F32)
                 return tuple(a + b for a, b in zip(carry, (part, *turned(part, other))))
 
             total, *kept = lax.fori_loop(1, chips, add_sum, (own, *turned(own, chip)))
@@ -359,16 +365,19 @@
             for unit in range(count):
                 part = made[:, unit * nvec : (unit + 1) * nvec].reshape(3, 8, nvec).astype(BF16)
                 for colour in range(3):
-                    rest[colour, group.seat, unit] = part[colour]
-
-            def send_rest(colour):
-                cell = rest.at[colour, group.seat]
-                remote(
-                    cell, cell, all_send, mate_recv.at[colour], group.mate_chip * 2 + core
-                ).start()
-                spread(cell, all_recv.at[group.index, colour], all_send, all_send)
-
-            each(0, 3, send_rest)
+                    rest[colour, core * owners + place, unit] = part[colour]
+
+            mate = half - depth + lax.rem(place + depth, owners)
+
+            def send_mate(colour):
+                cell = rest.at[colour, core * owners + place]
+                remote(cell, cell, all_send_b, mate_recv.at[colour], mate * 2 + core).start()
+
+            each(0, 3, send_mate)
+            each(
+                0, 3,
+                lambda colour: spread(rest.at[colour, core * owners + place], colour, all_send_b),
+            )
             return
         acc[:24, :] = made[:, :nvec]
         for i in range(len(fixed)):
@@ -385,17 +394,17 @@
 
         for colour in range(3):
             others = [plain[colour, :, slot * nvec : (slot + 1) * nvec] for slot in range(slots - 1)]
-            target = coeffs.at[colour, core, group.mine]
-            coeffs[colour, core, group.mine, 0] = merged(colour, chip)
+            target = coeffs.at[colour, place]
+            coeffs[colour, place, 0] = merged(colour, chip)
             for slot in range(slots - 1):
-                coeffs[colour, core, group.mine, slot + 1] = others[slot]
+                coeffs[colour, place, slot + 1] = others[slot]
 
             def send_coeffs(other, colour=colour, others=others, target=target):
                 ready[colour, other, 0] = merged(colour, other)
                 for slot in range(slots - 1):
                     ready[colour, other, slot + 1] = others[slot]
                 remote(
-                    ready.at[colour, other], target, all_send, all_recv.at[group.index, colour],
+                    ready.at[colour, other], target, all_send_a, all_recv.at[group.index, colour],
                     other * 2 + core,
                 ).start()
 
@@ -421,32 +430,36 @@
         if i == 0 and len(plan) > 1:
             build_all()
 
-    def relay(colour):
-        group = plan[0]
+    def relay(group, colour):
+        index = group.index
 
         def take(count):
-            landed(coeffs.at[colour, core, pl.ds(0, count)], all_recv.at[0, colour])
-
-        pl.when(group.owns)(lambda: take(group.owners - 1))
-        pl.when(jnp.logical_not(group.owns))(lambda: take(group.owners))
-        cells = coeffs.at[colour, core]
-        remote(cells, cells, fwd_send, fwd_recv.at[colour], partner).start()
+            pieces = (coeffs, rest)[index].at[colour, pl.ds(0, count)]
+            landed(pieces, all_recv.at[index, colour])
+
+        def run():
+            pl.when(central)(lambda: take(owners - 1 if index == 0 else owners - 2))
+            pl.when(jnp.logical_not(central))(lambda: take(owners))
+            if index == 0:
+                cells = coeffs.at[colour]
+            else:
+                cells = rest.at[colour, pl.ds(core * owners, owners)]
+            remote(
+                cells, cells, (fwd_send_a, fwd_send_b)[index], fwd_recv.at[index, colour], partner
+            ).start()
+
+        if index == 0:
+            pl.when(core == 1)(run)
+        else:
+            run()
 
     def rebuild(group, colour):
         height = group.width * slots * 8
         if group.index == 0:
-            landed(coeffs.at[colour, 1 - core], fwd_recv.at[colour])
-            lhs[: group.width] = coeffs[colour].reshape(group.width, slots, 8, nvec)
+            pl.when(core == 0)(lambda: landed(coeffs.at[colour], fwd_recv.at[0, colour]))
+            lhs[: group.width] = coeffs[colour]
         else:
-            for passes in range(2):
-                for owns in range(2):
-
-                    @pl.when((group.passes == (passes == 1)) & (group.owns == (owns == 1)))
-                    def _(count=2 * group.owners - passes - owns):
-                        landed(
-                            rest.at[colour, pl.ds(0, count)], all_recv.at[group.index, colour]
-                        )
-
+            landed(rest.at[colour, pl.ds((1 - core) * owners, owners)], fwd_recv.at[1, colour])
             table = rest[colour].reshape(group.width, slots + len(fixed), 8, nvec)
             still = table[:, 0].astype(F32)
             for i in range(len(fixed)):
@@ -491,7 +504,13 @@
             target = out.at[me, :, taken, picked]
 
         def send_pieces(t):
-            other = (1 - side if far else side) * half + lax.rem(chip + t, half)
+            if far:
+                step = t + lax.rem(chip, 2) * (1 - 2 * lax.rem(t, 2))
+                other = jnp.where(side == 0, chips - 1 - step, step)
+            else:
+                local = chip - side * half
+                step = jnp.where(t >= local, t + 1, t)
+                other = side * half + jnp.where(t == half - 1, local, step)
             chosen = jnp.dot(
                 source[base : base + height], onehot[other], preferred_element_type=F32
             )
@@ -526,49 +545,53 @@
                         staged.at[me, :, taken, picked], target, own_sem
                     ).start()
 
-        each(0 if far else 1, half if far else half + 1, send_pieces)
-
-    relay(0)
-    rebuild(plan[0], 0)
-    distribute(plan[0], (0,), True)
-    each(1, 3, relay)
-    pl.when(plan[1].passes)(functools.partial(pass_on, plan[1]))
-    each(1, 3, lambda colour: rebuild(plan[0], colour))
-    distribute(plan[0], (1, 2), True)
-    distribute(plan[0], (0, 1, 2), False)
-    rebuild(plan[1], 0)
-    distribute(plan[1], (0,), True)
-    each(1, 3, lambda colour: rebuild(plan[1], colour))
-    distribute(plan[1], (0, 1, 2), False)
-    distribute(plan[1], (1, 2), True)
-
-    owns = functools.reduce(jnp.logical_or, [group.owns for group in plan])
-    total_owners = 2 * sum(groups)
-
-    def sent_sums(count):
-        sent(summed.at[:, pl.ds(0, count)], chip_send)
-
-    sent(from_core, core_send)
-
-    pl.when(owns)(lambda: sent_sums(total_owners - 1))
-    pl.when(jnp.logical_not(owns))(lambda: sent_sums(total_owners))
-
-    line = 8 * (slots + len(fixed)) * nvec // length
-
-    @pl.when(plan[0].owns)
+        each(0, half, send_pieces)
+
+    early, late = plan
+    relay(early, 0)
+    rebuild(early, 0)
+    distribute(early, (0,), True)
+    each(1, 3, lambda colour: relay(early, colour))
+    each(1, 3, lambda colour: rebuild(early, colour))
+    pl.when(central)(lambda: each(0, 3, pass_on))
+    distribute(early, (1, 2), True)
+    relay(late, 0)
+    distribute(early, (0, 1, 2), False)
+    rebuild(late, 0)
+    distribute(late, (0,), True)
+    each(1, 3, lambda colour: relay(late, colour))
+    each(1, 3, lambda colour: rebuild(late, colour))
+    distribute(late, (0, 1, 2), False)
+    distribute(late, (1, 2), True)
+
+    def close(group):
+        pl.when(central)(lambda: sent(group.summed.at[:, pl.ds(0, owners - 1)], group.chip_send))
+        pl.when(jnp.logical_not(central))(lambda: sent(group.summed, group.chip_send))
+
+    @pl.when(core == 0)
     def _():
-        sent(ready.at[:, pl.ds(0, chips - 1)], all_send)
-
-    @pl.when(plan[1].owns)
+        sent(from_core_a, core_send_a)
+
+    @pl.when(core == 1)
     def _():
-        sent(eig.at[0, :, pl.ds(0, 2 * half * line)], all_send)
-
-    @pl.when(plan[1].passes)
+        close(early)
+        sent(coeffs, fwd_send_a)
+
+    sent(from_core_b, core_send_b)
+    close(late)
+    sent(rest.at[:, pl.ds(0, owners)], fwd_send_b)
+
+    @pl.when(early.owns)
     def _():
-        sent(eig.at[0, :, pl.ds(0, 2 * (half - 1) * line)], pass_send)
-        sent(rest.at[:, 0], partner_send)
-
-    sent(coeffs.at[:, 0], fwd_send)
+        sent(ready.at[:, pl.ds(0, chips - 1)], all_send_a)
+
+    @pl.when(late.owns)
+    def _():
+        line = 8 * (slots + len(fixed)) * nvec // length
+        sent(eig.at[0, :, pl.ds(0, half * line)], all_send_b)
+        for colour in range(3):
+            sent(prop.at[0, :, pl.ds(0, (half - 1) // 3)], pass_send.at[colour])
+
     sent(wanted.at[pl.ds(0, n - 1)], index_send)
     pltpu.make_async_copy(staged.at[0], staged.at[0], own_sem).wait()
     sent(staged.at[pl.ds(0, n - 1)], out_send)
@@ -583,16 +606,16 @@
     n = lax.axis_size("space")
     chips = n // 2
     piece = length // n
-    groups = (1,) * (columns % 8 // 4) + (2,) * (columns // 8)
+    depth = columns // 6
     fixed = tuple(
         p for p in range(1, NMOM)
         if MOMENTA[p][:2] == (0, 0) and EXTENT * EXTENT % (2 * length) == 0
     )
     moving = tuple(p for p in range(1, NMOM) if p not in fixed)
-    assert 4 * sum(groups) == columns and sum(groups) <= chips // 2
+    assert 6 * depth == columns and depth <= chips // 2 and (chips // 2 - 1) % 3 == 0
     slots = 1 + len(moving)
-    owners = 2 * sum(groups)
-    assert len(groups) == 2 and 8 * (slots + len(fixed)) * nvec % length == 0
+    owners = 2 * depth
+    assert 8 * (slots + len(fixed)) * nvec == 4 * length
     cell = (slots, 8, nvec)
     direct = piece % 128 == 0
     out_shape = (2, 3, columns, 4, length) if direct else (n, 2, 3, columns, 4, piece)
@@ -602,7 +625,7 @@
     dma = pltpu.SemaphoreType.DMA
     gathered = pl.pallas_call(
         functools.partial(
-            kernel, n, groups, columns, 1.0 / math.sqrt(3.0 * length * n),
+            kernel, n, depth, columns, 1.0 / math.sqrt(3.0 * length * n),
             1.0 / math.sqrt(NMOM * nvec), length, moving, fixed, direct,
         ),
         out_shape=pltpu.VMEM(out_shape, BF16),
@@ -618,20 +641,24 @@
             pltpu.VMEM((2 * len(moving), length), F32),
             pltpu.VMEM((2 * max(len(fixed), 1), chips, 1, nvec), F32),
             pltpu.VMEM((24 * (1 + len(fixed)), nvec), F32),
+            pltpu.VMEM((3, 1, owners) + cell, F32),
             pltpu.VMEM((3, 2, owners) + cell, F32),
             pltpu.VMEM((3, owners) + cell, F32),
+            pltpu.VMEM((3, owners) + cell, F32),
+            pltpu.VMEM((3, owners) + cell, BF16),
             pltpu.VMEM((3, owners) + cell, BF16),
             pltpu.VMEM((3, chips) + cell, BF16),
             pltpu.VMEM((3, chips) + cell, BF16),
-            pltpu.VMEM((3, 2, 2 * groups[0]) + cell, BF16),
-            pltpu.VMEM((3, 4 * groups[1], slots + len(fixed), 8, nvec), BF16),
-            pltpu.VMEM((4 * max(groups), slots, 8, nvec), BF16),
-            pltpu.VMEM((12 * 8 * max(groups), length), BF16),
+            pltpu.VMEM((3, chips) + cell, BF16),
+            pltpu.VMEM((3, owners) + cell, BF16),
+            pltpu.VMEM((3, 2 * owners, slots + len(fixed), 8, nvec), BF16),
+            pltpu.VMEM((2 * owners, slots, 8, nvec), BF16),
+            pltpu.VMEM((3 * 8 * 2 * owners, length), BF16),
             pltpu.VMEM((n, 1, piece), jnp.int32),
             pltpu.VMEM((chips, length, 2 * piece), BF16),
             pltpu.VMEM((n, 2, 3, columns, 4, piece), BF16),
-            dma((16,)), dma((len(groups), 3)), dma((3,)), dma((len(groups), 3)), dma((3,)), dma((3,)),
-            dma((11,)),
+            dma((16,)), dma((2, 3)), dma((2, 3)), dma((2, 3)), dma((2, 3)), dma((3,)), dma((3,)),
+            dma((13,)),
         ],
         compiler_params=pltpu.CompilerParams(
             collective_id=0, has_side_effects=True, vmem_limit_bytes=int(48 * 2**20)

time: 48.4 us -> 45.8 us (0.946)
  the two profiles are of different devices: /device:TPU:0 before, /device:TPU:9 now
where the time goes in v6:
time: 45.8 us; the launch traced here: 45.7 us
  Pallas kernels  44 us (96%)
  local copies, waits for them, and re-layouts  1.02 us (2%)
  between operations  0.66 us (1%)
    pallas_call x1, Pallas kernels, on_device(): pl.pallas_call(functools.partial(kernel, n, depth, columns, 1.0 / math.sq...  44 us
    unnamed x1, local copies, waits for them, and re-layouts  1.02 us

profile of v6, /device:TPU:9, one launch (start us, length us, event | category | flops | bytes accessed | tf_op | source)
XLA Modules:
  0.0 45.7 jit_solution(7724960049657675976)
XLA Ops:
  0.7 44.0 %shard_map.73 = bf16[2,3,12,4,2048]{4,3,2,1,0:T(4,128)(2,1)S(1)} custom-call(bf16[2,3,12,4,2048]{4,3,2,1,0:T(4,128)(2,1)} %bitcast.8, bf16[2,3,256,2048]{3,2,1,0:T(8,128)(2,1)} %eig_hbm.1, s32[1,1]{1,0:T(1,128)} %bitcast.6.sink, f32[128,2,256]{2,1,0:T(2,128)} %table_hbm.1, s32[3,48]{1,0:T(4,128)} %bitcast.10, s32[1,48]{1,0:T(1,128)} %bitcast.11, ...), custom_call_target="tpu_custom_call" | custom-call | tf_op jit(solution)/shard_map/pallas_call | solution.py:626
  44.7 1.0 %copy.9 = bf16[2,3,4,12,2048]{4,2,3,1,0:T(4,128)(2,1)} copy(bf16[2,3,4,12,2048]{4,2,3,1,0:T(4,128)(2,1)S(1)} %bitcast.7) | data formatting | bytes 2359296

commit v7 on v6

--- a/solution.py
+++ b/solution.py
@@ -423,13 +423,6 @@
         landed(wanted.at[pl.ds(0, n - 1)], index_recv)
         each(0, chips, build)
 
-    for i, group in enumerate(plan):
-        if i == 0 and len(plan) == 1:
-            build_all()
-        pl.when(group.owns)(functools.partial(contract, group))
-        if i == 0 and len(plan) > 1:
-            build_all()
-
     def relay(group, colour):
         index = group.index
 
@@ -492,7 +485,7 @@
 
         each(0, steps, step)
 
-    def distribute(group, colours, far):
+    def distribute(group, colours, far, last=False):
         picked = pl.ds(group.left, group.width)
         taken = pl.ds(colours[0], len(colours))
         height = 8 * group.width * len(colours)
@@ -505,7 +498,10 @@
 
         def send_pieces(t):
             if far:
-                step = t + lax.rem(chip, 2) * (1 - 2 * lax.rem(t, 2))
+                swap = 1 - 2 * lax.rem(t, 2)
+                if last:
+                    swap = jnp.where(t < half - 2, swap, 0)
+                step = t + lax.rem(chip, 2) * swap
                 other = jnp.where(side == 0, chips - 1 - step, step)
             else:
                 local = chip - side * half
@@ -548,13 +544,17 @@
         each(0, half, send_pieces)
 
     early, late = plan
+    pl.when(early.owns)(functools.partial(contract, early))
+    build_all()
     relay(early, 0)
+    pl.when(late.owns)(functools.partial(contract, late))
     rebuild(early, 0)
     distribute(early, (0,), True)
     each(1, 3, lambda colour: relay(early, colour))
+    pl.when(central)(lambda: pass_on(0))
     each(1, 3, lambda colour: rebuild(early, colour))
-    pl.when(central)(lambda: each(0, 3, pass_on))
     distribute(early, (1, 2), True)
+    pl.when(central)(lambda: each(1, 3, pass_on))
     relay(late, 0)
     distribute(early, (0, 1, 2), False)
     rebuild(late, 0)
@@ -562,7 +562,7 @@
     each(1, 3, lambda colour: relay(late, colour))
     each(1, 3, lambda colour: rebuild(late, colour))
     distribute(late, (0, 1, 2), False)
-    distribute(late, (1, 2), True)
+    distribute(late, (1, 2), True, True)
 
     def close(group):
         pl.when(central)(lambda: sent(group.summed.at[:, pl.ds(0, owners - 1)], group.chip_send))

time: 45.8 us -> 45.4 us (level)
  the two profiles are of different devices: /device:TPU:9 before, /device:TPU:15 now
where the time goes in v7:
time: 45.4 us; the launch traced here: 45.3 us
  Pallas kernels  43.6 us (96%)
  local copies, waits for them, and re-layouts  1.02 us (2%)
  between operations  0.66 us (1%)
    pallas_call x1, Pallas kernels, on_device(): pl.pallas_call(functools.partial(kernel, n, depth, columns, 1.0 / math.sq...  43.6 us
    unnamed x1, local copies, waits for them, and re-layouts  1.02 us

profile of v7, /device:TPU:15, one launch (start us, length us, event | category | flops | bytes accessed | tf_op | source)
XLA Modules:
  0.0 45.3 jit_solution(5528664290697696163)
XLA Ops:
  0.7 43.6 %shard_map.73 = bf16[2,3,12,4,2048]{4,3,2,1,0:T(4,128)(2,1)S(1)} custom-call(bf16[2,3,12,4,2048]{4,3,2,1,0:T(4,128)(2,1)} %bitcast.8, bf16[2,3,256,2048]{3,2,1,0:T(8,128)(2,1)} %eig_hbm.1, s32[1,1]{1,0:T(1,128)} %bitcast.6.sink, f32[128,2,256]{2,1,0:T(2,128)} %table_hbm.1, s32[3,48]{1,0:T(4,128)} %bitcast.10, s32[1,48]{1,0:T(1,128)} %bitcast.11, ...), custom_call_target="tpu_custom_call" | custom-call | tf_op jit(solution)/shard_map/pallas_call | solution.py:626
  44.3 1.0 %copy.9 = bf16[2,3,4,12,2048]{4,2,3,1,0:T(4,128)(2,1)} copy(bf16[2,3,4,12,2048]{4,2,3,1,0:T(4,128)(2,1)S(1)} %bitcast.7) | data formatting | bytes 2359296

commit v8 on v7

--- a/solution.py
+++ b/solution.py
@@ -96,6 +96,7 @@
         def __init__(self, index, left, cores, *refs):
             self.index, self.left, self.cores = index, left, cores
             self.width = owners * len(cores)
+            self.base = 3 * 8 * owners * index
             self.owns = central & (core == 1) if len(cores) == 1 else central
             self.row = core if len(cores) == 2 else 0
             self.blocks, self.from_core, self.summed, self.from_chips = refs[:4]
@@ -461,7 +462,7 @@
                 still = still + turn[2 * i + 1, chip] * swap_halves(turned)
             lhs[: group.width, 0] = still.astype(BF16)
             lhs[: group.width, 1:] = table[:, 1:slots]
-        base = pl.multiple_of(colour * 8 * group.width, 8 * group.width)
+        base = pl.multiple_of(group.base + colour * 8 * group.width, 8 * owners)
 
         def step(step):
             sites = pl.ds(pl.multiple_of(step * chunk, chunk), chunk)
@@ -489,7 +490,7 @@
         picked = pl.ds(group.left, group.width)
         taken = pl.ds(colours[0], len(colours))
         height = 8 * group.width * len(colours)
-        base = 8 * group.width * colours[0]
+        base = group.base + 8 * group.width * colours[0]
         if direct:
             lanes = pl.ds(pl.multiple_of(me * piece, piece), piece)
             target = out.at[:, taken, picked, :, lanes]
@@ -500,7 +501,7 @@
             if far:
                 swap = 1 - 2 * lax.rem(t, 2)
                 if last:
-                    swap = jnp.where(t < half - 2, swap, 0)
+                    swap = jnp.where((side == 0) | (t < half - 2), swap, 0)
                 step = t + lax.rem(chip, 2) * swap
                 other = jnp.where(side == 0, chips - 1 - step, step)
             else:
@@ -556,9 +557,9 @@
     distribute(early, (1, 2), True)
     pl.when(central)(lambda: each(1, 3, pass_on))
     relay(late, 0)
-    distribute(early, (0, 1, 2), False)
     rebuild(late, 0)
     distribute(late, (0,), True)
+    distribute(early, (0, 1, 2), False)
     each(1, 3, lambda colour: relay(late, colour))
     each(1, 3, lambda colour: rebuild(late, colour))
     distribute(late, (0, 1, 2), False)
@@ -653,7 +654,7 @@
             pltpu.VMEM((3, owners) + cell, BF16),
             pltpu.VMEM((3, 2 * owners, slots + len(fixed), 8, nvec), BF16),
             pltpu.VMEM((2 * owners, slots, 8, nvec), BF16),
-            pltpu.VMEM((3 * 8 * 2 * owners, length), BF16),
+            pltpu.VMEM((3 * 8 * 3 * owners, length), BF16),
             pltpu.VMEM((n, 1, piece), jnp.int32),
             pltpu.VMEM((chips, length, 2 * piece), BF16),
             pltpu.VMEM((n, 2, 3, columns, 4, piece), BF16),

time: 45.4 us -> 45.4 us (level)
  the two profiles are of different devices: /device:TPU:15 before, /device:TPU:0 now
where the time goes in v8:
time: 45.4 us; the launch traced here: 44.6 us
  Pallas kernels  42.9 us (94%)
  local copies, waits for them, and re-layouts  1.02 us (2%)
  between operations  0.66 us (1%)
    pallas_call x1, Pallas kernels, on_device(): pl.pallas_call(functools.partial(kernel, n, depth, columns, 1.0 / math.sq...  42.9 us
    unnamed x1, local copies, waits for them, and re-layouts  1.02 us

profile of v8, /device:TPU:0, one launch (start us, length us, event | category | flops | bytes accessed | tf_op | source)
XLA Modules:
  0.0 44.6 jit_solution(10502752650568743554)
XLA Ops:
  0.7 42.9 %shard_map.73 = bf16[2,3,12,4,2048]{4,3,2,1,0:T(4,128)(2,1)S(1)} custom-call(bf16[2,3,12,4,2048]{4,3,2,1,0:T(4,128)(2,1)} %bitcast.8, bf16[2,3,256,2048]{3,2,1,0:T(8,128)(2,1)} %eig_hbm.1, s32[1,1]{1,0:T(1,128)} %bitcast.6.sink, f32[128,2,256]{2,1,0:T(2,128)} %table_hbm.1, s32[3,48]{1,0:T(4,128)} %bitcast.10, s32[1,48]{1,0:T(1,128)} %bitcast.11, ...), custom_call_target="tpu_custom_call" | custom-call | tf_op jit(solution)/shard_map/pallas_call | solution.py:627
  43.5 1.0 %copy.9 = bf16[2,3,4,12,2048]{4,2,3,1,0:T(4,128)(2,1)} copy(bf16[2,3,4,12,2048]{4,2,3,1,0:T(4,128)(2,1)S(1)} %bitcast.7) | data formatting | bytes 2359296
